TPU v7x, 32 devices: a whole 2x2x4 slice. The times are simulated.
32 devices in a mesh: grp: 2 (over core), row: 4 (over z), col: 4 (over y, x).
Axes of the slice: x: 2, y: 2, z: 4, core: 2. Of those that a mesh axis runs over, the one named last changes fastest.
Arguments:
- ainv_anc: bfloat16 [6144, 6144], P(('grp', 'row'), 'col'), may hold values from -12 to 12
- l_upper: bfloat16 [6144, 1024], P(('grp', 'row'), 'col'), may hold values from -0.078125 to 0.078125
- mask_upper: int32 [4, 24], replicated, may hold values from 0 to 1, as said below
- dinv_upper: float32 [256, 1024], P(None, 'col'), may hold values from -6 to 6
- l_lower: bfloat16 [6144, 1024], P(('grp', 'row'), 'col'), may hold values from -0.078125 to 0.078125
- mask_lower: int32 [4, 24], replicated, may hold values from 0 to 1, as said below
- parent: int32 [4], replicated, may hold values from 0 to 3
- lp_lower: bfloat16 [256, 1024], P(None, 'col'), may hold values from -0.375 to 0.375
- dinv_lower: float32 [256, 1024], P(None, 'col'), may hold values from -6 to 6
Outputs:
- x_upper: bfloat16 [6144, 1024], P(('grp', 'row'), 'col')
- diag_upper: bfloat16 [256, 1024], P(None, 'col')
- y_lower: bfloat16 [6144, 1024], P(('grp', 'row'), 'col')
- y_parent: bfloat16 [256, 1024], P(None, 'col')
- diag_lower: bfloat16 [256, 1024], P(None, 'col')
Inputs may be any that keep to these rules, and one draw needn't show every extreme that they name: mask_upper[u, a] is 1 where ancestor block a lies in the structure of upper supernode u. mask_lower[l, a] is 1 where ancestor block a lies in the structure of lower supernode l. parent[l] is the upper supernode whose columns hold lower supernode l's parent block.
All inputs are finite; a program needn't handle non-finite values.
Results may differ from a plain program's by a relative error of at most 0.0095.
Values may be sent and summed in bfloat16 or wider, within the bound.
A program may use at most 128 MiB of HBM per device.

v0:
```python
import functools

import jax
import jax.numpy as jnp
from jax import lax
from jax.experimental import pallas as pl
from jax.experimental.pallas import tpu as pltpu
from jax.sharding import PartitionSpec as P

B = 256
MESH = pl.DeviceIdType.MESH
BF = jnp.bfloat16
F32 = jnp.float32


def tdot(a, b):
    return lax.dot_general(a, b, (((0,), (0,)), ((), ())), preferred_element_type=F32)


def kernel(
    G, R, C,
    a_ref, lu_ref, mu_ref, du_ref, ll_ref, ml_ref, par_ref, lp_ref, dl_ref,
    x_ref, diagu_ref, y_ref, yp_ref, diagl_ref,
    zbuf, col, part, near, sent, last, acc, xall, rhs, lum, llm, part3, red, dufull, dpar,
    ypfull, back, dlfull,
    pre_ss, z_ss, z_rs, p_ss, c_rs, r_ss, n_ss, n_rs, l_ss, l_rs, x_ss, x_rs, xy_ss,
    red_ss, red_rs, d_ss, d_rs, dp_ss, dp_rs, y_ss, y_rs, o_ss, o_rs,
):
    g, z, c = lax.axis_index("grp"), lax.axis_index("row"), lax.axis_index("col")
    n = G * R
    q = n // C
    CX = C // G
    y, x = lax.div(c, CX), lax.rem(c, CX)
    r = g * R + z
    h = lu_ref.shape[0]
    W = hb = h // B
    S = B // n
    panels = (lu_ref, ll_ref)
    masks = (mu_ref, ml_ref)
    primary = y == g

    def rdev(i):
        return (lax.div(i, R), lax.rem(i, R), c)

    def copy(src, dst, ss, rs, dev):
        return pltpu.make_async_remote_copy(
            src_ref=src, dst_ref=dst, send_sem=ss, recv_sem=rs, device_id=dev, device_id_type=MESH
        )

    barrier = pltpu.get_barrier_semaphore()
    for o in range(1, n):
        pl.semaphore_signal(barrier, inc=1, device_id=rdev(lax.rem(r + o, n)), device_id_type=MESH)
    for o in range(1, C):
        pl.semaphore_signal(
            barrier, inc=1, device_id=(g, z, lax.rem(c + o, C)), device_id_type=MESH
        )
    pl.semaphore_wait(barrier, n - 1 + C - 1)

    def cutr(w):
        return pl.ds(w * (h // W), h // W)

    def pre_copy(p, w):
        return copy(
            panels[p].at[cutr(w), :], zbuf.at[p, z, y, cutr(w), :], pre_ss.at[p, w],
            z_rs.at[p, z, y, w], (g, z, g * CX + x),
        )

    def row_copy(p, z0, yy, side, w, own=False):
        to = z + 1 if side == 0 else z - 1
        at = zbuf.at[p, z0, yy, cutr(w), :]
        return copy(
            panels[p].at[cutr(w), :] if own else at, at, z_ss.at[p, z0, yy, side, w],
            z_rs.at[p, z0, yy, w], (g, to, c),
        )

    def piece(p, z0, yy, w, own):
        return panels[p].at[cutr(w), :] if own else zbuf.at[p, z0, yy, cutr(w), :]

    def plane_copy(p, z0, yy, w, own=False):
        r0 = g * R + z0
        u = yy * CX + x
        j = lax.rem(r0, q)
        return copy(
            piece(p, z0, yy, w, own), col.at[p, j, u, cutr(w), :], p_ss.at[p, z0, yy, w],
            c_rs.at[p, j, u, w], (g, z, lax.div(r0, q)),
        )

    def relay_copy(p, j, u, w):
        at = col.at[p, j, u, cutr(w), :]
        return copy(at, at, r_ss.at[p, j, u, w], c_rs.at[p, j, u, w], (1 - g, z, c))

    def to_plane(p, z0, yy, w, own):
        r0 = g * R + z0
        d = lax.div(r0, q)

        @pl.when(d == c)
        def _():
            j = lax.rem(r0, q)
            u = yy * CX + x
            pltpu.make_async_copy(
                piece(p, z0, yy, w, own), col.at[p, j, u, cutr(w), :], c_rs.at[p, j, u, w]
            ).start()

        @pl.when(d != c)
        def _():
            plane_copy(p, z0, yy, w, own).start()

    def pass_on(p, z0, yy, sides, w, own=False):
        if 0 in sides:
            @pl.when(z < R - 1)
            def _():
                row_copy(p, z0, yy, 0, w, own).start()

        if 1 in sides:
            @pl.when(z > 0)
            def _():
                row_copy(p, z0, yy, 1, w, own).start()

        to_plane(p, z0, yy, w, own)

    def start_own(p):
        for w in range(W):
            pass_on(p, z, g, (0, 1), w, True)
        for w in range(W):
            row_copy(p, z, 1 - g, 0, w).wait_recv()
            pass_on(p, z, 1 - g, (0, 1), w)

    def relay(p, z0):
        r0 = g * R + z0

        @pl.when(lax.div(r0, q) == c)
        def _():
            j = lax.rem(r0, q)
            for o in range(CX):
                for yy in range(G):
                    for w in range(W):
                        u = yy * CX + lax.rem(x + o, CX)
                        relay_copy(p, j, u, w).wait_recv()
                        relay_copy(p, j, u, w).start()

    def relay_step(p, s):
        if s < 0:
            return
        if s == 0:
            relay(p, z)
            return

        @pl.when(z - s >= 0)
        def _():
            relay(p, z - s)

        @pl.when(z + s < R)
        def _():
            relay(p, z + s)

    def row_step(p, s):
        zl, zr = z - s, z + s
        for i in range(G):
            for w in range(W):
                yy = lax.rem(g + i, G)

                @pl.when(zl >= 0)
                def _():
                    row_copy(p, zl, yy, 0, w).wait_recv()
                    pass_on(p, zl, yy, (0,), w)

                @pl.when(zr < R)
                def _():
                    row_copy(p, zr, yy, 1, w).wait_recv()
                    pass_on(p, zr, yy, (1,), w)

        relay_step(p, s - 2)

    def near_copy(p, ux):
        return copy(
            part.at[p, ux], near.at[p, ux], n_ss.at[p, ux], n_rs.at[p, ux], (g, z, (1 - y) * CX + x)
        )

    def last_copy(p, ux):
        return copy(
            sent.at[p, ux], last.at[p, x], l_ss.at[p, ux], l_rs.at[p, x], (g, z, y * CX + ux)
        )

    def products(p):
        @pl.when(primary)
        def _():
            for s in range(max(R - 2, 0), R):
                relay_step(p, s)

        @pl.when(jnp.logical_not(primary))
        def _():
            for j in range(q):
                for u in range(C):
                    for w in range(W):
                        relay_copy(p, j, u, w).wait_recv()

        offsets = list(range(1, CX)) + [0]
        for near_side, o in [(True, o) for o in offsets] + [(False, o) for o in offsets]:
            ux = lax.rem(x + o, CX)
            u = ((1 - y) if near_side else y) * CX + ux

            @pl.loop(0, q * hb)
            def _(k):
                j, t = lax.div(k, hb), lax.rem(k, hb)
                keep = masks[p][u, c * q * hb + k] > 0
                rows = pl.ds(pl.multiple_of(t * B, B), B)
                blk = col[p, j, u, rows, :]
                rhs[pl.ds(pl.multiple_of(k * B, B), B), :] = jnp.where(
                    keep, blk, jnp.zeros_like(blk)
                )

            @pl.loop(0, hb)
            def _(t):
                rows = pl.ds(pl.multiple_of(t * B, B), B)
                v = jnp.dot(a_ref[rows, :], rhs[...], preferred_element_type=F32)
                if near_side:
                    part[p, ux, rows, :] = v.astype(BF)
                else:
                    acc[p, ux, rows, :] = v

            if near_side:
                near_copy(p, ux).start()

    def second(p):
        for o in range(1, CX):
            ux = lax.rem(x + o, CX)
            near_copy(p, ux).wait_recv()

            @pl.loop(0, hb)
            def _(t):
                rows = pl.ds(pl.multiple_of(t * B, B), B)
                sent[p, ux, rows, :] = (
                    acc[p, ux, rows, :] + near[p, ux, rows, :].astype(F32)
                ).astype(BF)

            last_copy(p, ux).start()

    def wait_parts(p):
        near_copy(p, x).wait_recv()
        for o in range(1, CX):
            ux = lax.rem(x + o, CX)
            copy(
                last.at[p, ux], last.at[p, ux], l_ss.at[p, ux], l_rs.at[p, ux], (g, z, y * CX + ux)
            ).wait_recv()

    def total(p, rows):
        v = acc[p, x, rows, :] + near[p, x, rows, :].astype(F32)
        for o in range(1, CX):
            v = v + last[p, lax.rem(x + o, CX), rows, :].astype(F32)
        return v

    def red_copy(k, o):
        i = lax.rem(r + o, n)
        return copy(
            part3.at[k, pl.ds(pl.multiple_of(i * S, S), S), :], red.at[k, r],
            red_ss.at[k, o], red_rs.at[k, r], rdev(i),
        )

    def send_sum(k):
        red[k, r] = part3[k, pl.ds(pl.multiple_of(r * S, S), S), :]
        for o in range(1, n):
            red_copy(k, o).start()

    def take_sum(k):
        for o in range(1, n):
            s = lax.rem(r + o, n)
            copy(
                red.at[k, s], red.at[k, s], red_ss.at[k, o], red_rs.at[k, s], rdev(s)
            ).wait_recv()
        v = red[k, 0].astype(F32)
        for i in range(1, n):
            v = v + red[k, i].astype(F32)
        return v

    mine = pl.ds(pl.multiple_of(r * S, S), S)

    def spread_copy(buf, ss, rs, o):
        return copy(buf.at[mine, :], buf.at[mine, :], ss.at[o], rs.at[r], rdev(lax.rem(r + o, n)))

    def spread(buf, ss, rs):
        for o in range(1, n):
            spread_copy(buf, ss, rs, o).start()

    def gathered(buf, ss, rs):
        for o in range(1, n):
            s = lax.rem(r + o, n)
            at = buf.at[pl.ds(pl.multiple_of(s * S, S), S), :]
            copy(at, at, ss.at[o], rs.at[s], rdev(s)).wait_recv()

    def xn_copy():
        return copy(
            xall.at[c], xall.at[c], x_ss.at[0], x_rs.at[c], (g, z, (1 - y) * CX + x)
        )

    def xr_copy(o, yy):
        u = yy * CX + x
        return copy(
            xall.at[u], xall.at[u], xy_ss.at[o, yy], x_rs.at[u],
            (g, z, y * CX + lax.rem(x + o, CX)),
        )

    def wait_x(u):
        copy(xall.at[u], xall.at[u], x_ss.at[0], x_rs.at[u], (g, z, (1 - y) * CX + x)).wait_recv()

    def dp_copy(o):
        return copy(dpar.at[c], dpar.at[c], dp_ss.at[o], dp_rs.at[c], (g, z, lax.rem(c + o, C)))

    @pl.when(primary)
    def _():
        start_own(0)

    @pl.when(jnp.logical_not(primary))
    def _():
        for p in range(2):
            for w in range(W):
                pre_copy(p, w).start()

    @pl.loop(0, hb)
    def _(t):
        rows = pl.ds(pl.multiple_of(t * B, B), B)
        ub, lb = lu_ref[rows, :], ll_ref[rows, :]
        lum[rows, :] = jnp.where(mu_ref[c, r * hb + t] > 0, ub, jnp.zeros_like(ub))
        llm[rows, :] = jnp.where(ml_ref[c, r * hb + t] > 0, lb, jnp.zeros_like(lb))

    @pl.when(primary)
    def _():
        for s in range(1, R):
            row_step(0, s)
        start_own(1)
        row_step(1, 1)

    products(0)

    @pl.when(primary)
    def _():
        row_step(1, 2)

    second(0)

    @pl.when(primary)
    def _():
        for s in range(3, R):
            row_step(1, s)

    wait_parts(0)

    @pl.loop(0, hb)
    def _(t):
        rows = pl.ds(pl.multiple_of(t * B, B), B)
        v = (-total(0, rows)).astype(BF)
        xall[c, rows, :] = v
        x_ref[rows, :] = v

    xn_copy().start()
    for o in range(1, CX):
        xr_copy(o, y).start()

    products(1)

    wait_x((1 - y) * CX + x)
    for o in range(1, CX):
        xr_copy(o, 1 - y).start()
    part3[0] = tdot(lum[...], x_ref[...]).astype(BF)
    send_sum(0)
    second(1)
    for o in range(1, CX):
        for yy in range(G):
            wait_x(yy * CX + lax.rem(x + o, CX))
    here = par_ref[c]
    part3[1] = tdot(xall[here], llm[...]).astype(BF)
    send_sum(1)

    dslice = (du_ref[mine, :] - take_sum(0)).astype(BF)
    dufull[mine, :] = dslice
    dpar[c] = dslice
    for o in range(1, C):
        dp_copy(o).start()
    spread(dufull, d_ss, d_rs)

    @pl.loop(0, hb)
    def _(t):
        rows = pl.ds(pl.multiple_of(t * B, B), B)
        acc[1, x, rows, :] += jnp.dot(xall[here, rows, :], lp_ref[...], preferred_element_type=F32)

    for o in range(1, C):
        s = lax.rem(c + o, C)
        copy(dpar.at[s], dpar.at[s], dp_ss.at[o], dp_rs.at[s], (g, z, s)).wait_recv()
    terms = jnp.dot(dpar[here], lp_ref[...], preferred_element_type=F32)
    ypfull[mine, :] = (-(take_sum(1) + terms)).astype(BF)
    spread(ypfull, y_ss, y_rs)

    wait_parts(1)

    @pl.loop(0, hb)
    def _(t):
        rows = pl.ds(pl.multiple_of(t * B, B), B)
        y_ref[rows, :] = (-total(1, rows)).astype(BF)

    part3[2] = tdot(llm[...], y_ref[...]).astype(BF)
    send_sum(2)
    gathered(ypfull, y_ss, y_rs)
    back[...] = tdot(lp_ref[...], ypfull[...])
    yp_ref[...] = ypfull[...]
    gathered(dufull, d_ss, d_rs)
    diagu_ref[...] = dufull[...]
    dlfull[mine, :] = (dl_ref[mine, :] - take_sum(2) - back[mine, :]).astype(BF)
    spread(dlfull, o_ss, o_rs)
    gathered(dlfull, o_ss, o_rs)
    diagl_ref[...] = dlfull[...]

    for p in range(2):
        @pl.when(primary)
        def _():
            for z0 in range(R):
                for yy in range(G):
                    for w in range(W):
                        @pl.when(jnp.logical_and(z0 <= z, z < R - 1))
                        def _():
                            row_copy(p, z0, yy, 0, w).wait_send()

                        @pl.when(jnp.logical_and(z0 >= z, z > 0))
                        def _():
                            row_copy(p, z0, yy, 1, w).wait_send()

                        @pl.when(lax.div(g * R + z0, q) != c)
                        def _():
                            plane_copy(p, z0, yy, w).wait_send()

            for j in range(q):
                for u in range(C):
                    for w in range(W):
                        relay_copy(p, j, u, w).wait_send()

        @pl.when(jnp.logical_not(primary))
        def _():
            for w in range(W):
                pre_copy(p, w).wait_send()

        for ux in range(CX):
            near_copy(p, ux).wait_send()
        for o in range(1, CX):
            last_copy(p, lax.rem(x + o, CX)).wait_send()
    xn_copy().wait_send()
    for o in range(1, CX):
        for yy in range(G):
            xr_copy(o, yy).wait_send()
    for o in range(1, C):
        dp_copy(o).wait_send()
    for o in range(1, n):
        for k in range(3):
            red_copy(k, o).wait_send()
        spread_copy(dufull, d_ss, d_rs, o).wait_send()
        spread_copy(ypfull, y_ss, y_rs, o).wait_send()
        spread_copy(dlfull, o_ss, o_rs, o).wait_send()


def on_device(G, R, C, a, lu, mu, du, ll, ml, par, lp, dl):
    h = lu.shape[0]
    n = G * R
    q = n // C
    S = B // n
    CX = C // G
    W = h // B
    vm = pl.BlockSpec(memory_space=pltpu.VMEM)
    sm = pl.BlockSpec(memory_space=pltpu.SMEM)
    dma = pltpu.SemaphoreType.DMA
    small = jax.ShapeDtypeStruct((B, B), BF)
    tall = jax.ShapeDtypeStruct((h, B), BF)
    return pl.pallas_call(
        functools.partial(kernel, G, R, C),
        out_shape=(tall, small, tall, small, small),
        in_specs=[vm, vm, sm, vm, vm, sm, sm, vm, vm],
        out_specs=(vm,) * 5,
        scratch_shapes=[
            pltpu.VMEM((2, R, G, h, B), BF),
            pltpu.VMEM((2, q, C, h, B), BF),
            pltpu.VMEM((2, CX, h, B), BF),
            pltpu.VMEM((2, CX, h, B), BF),
            pltpu.VMEM((2, CX, h, B), BF),
            pltpu.VMEM((2, CX, h, B), BF),
            pltpu.VMEM((2, CX, h, B), F32),
            pltpu.VMEM((C, h, B), BF),
            pltpu.VMEM((q * h, B), BF),
            pltpu.VMEM((h, B), BF),
            pltpu.VMEM((h, B), BF),
            pltpu.VMEM((3, B, B), BF),
            pltpu.VMEM((3, n, S, B), BF),
            pltpu.VMEM((B, B), BF),
            pltpu.VMEM((C, S, B), BF),
            pltpu.VMEM((B, B), BF),
            pltpu.VMEM((B, B), F32),
            pltpu.VMEM((B, B), BF),
            dma((2, W)), dma((2, R, G, 2, W)), dma((2, R, G, W)), dma((2, R, G, W)),
            dma((2, q, C, W)), dma((2, q, C, W)), dma((2, CX)), dma((2, CX)), dma((2, CX)), dma((2, CX)),
            dma((1,)), dma((C,)), dma((CX, G)), dma((3, n)), dma((3, n)),
            dma((n,)), dma((n,)), dma((C,)), dma((C,)), dma((n,)), dma((n,)), dma((n,)), dma((n,)),
        ],
        compiler_params=pltpu.CompilerParams(
            collective_id=0, has_side_effects=True, vmem_limit_bytes=60 * 1024 * 1024
        ),
    )(a, lu, mu, du, ll, ml, par, lp, dl)


def solution(mesh):
    tall, wide = P(("grp", "row"), "col"), P(None, "col")
    return jax.shard_map(
        functools.partial(
            on_device, mesh.shape["grp"], mesh.shape["row"], mesh.shape["col"]
        ),
        mesh=mesh,
        in_specs=(tall, tall, P(), wide, tall, P(), P(), wide, wide),
        out_specs=(tall, wide, tall, wide, wide),
        check_vma=False,
    )
```

profile of v0, /device:TPU:0, one launch (start us, length us, event | category | flops | bytes accessed | tf_op | source)
XLA Modules:
  0.0 133.4 jit_solution(13545913517849412534)
XLA Ops:
  0.6 124.5 %shard_map.128 = (bf16[768,256]{1,0:T(8,128)(2,1)}, bf16[256,256]{1,0:T(8,128)(2,1)}, bf16[768,256]{1,0:T(8,128)(2,1)}, bf16[256,256]{1,0:T(8,128)(2,1)}, bf16[256,256]{1,0:T(8,128)(2,1)}) custom-call(bf16[768,1536]{1,0:T(8,128)(2,1)} %a_ref.1, bf16[768,256]{1,0:T(8,128)(2,1)} %lu_ref.1, s32[4,24]{1,0:T(4,128)} %mu_ref.1, f32[256,256]{1,0:T(8,128)} %du_ref.1, ...), custom_call_target="tpu_custom_call" | custom-call | tf_op jit(solution)/shard_map/pallas_call | solution.py:469
  125.1 1.8 %copy.19 = bf16[768,256]{1,0:T(8,128)(2,1)} copy(bf16[768,256]{1,0:T(8,128)(2,1)} %get-tuple-element.10) | data formatting | bytes 786432
  126.9 1.6 %copy.20 = bf16[256,256]{1,0:T(8,128)(2,1)} copy(bf16[256,256]{1,0:T(8,128)(2,1)} %get-tuple-element.11) | data formatting | bytes 262144
  128.5 1.8 %copy.21 = bf16[768,256]{1,0:T(8,128)(2,1)} copy(bf16[768,256]{1,0:T(8,128)(2,1)} %get-tuple-element.12) | data formatting | bytes 786432
  130.3 1.6 %copy.22 = bf16[256,256]{1,0:T(8,128)(2,1)} copy(bf16[256,256]{1,0:T(8,128)(2,1)} %get-tuple-element.13) | data formatting | bytes 262144
  131.8 1.6 %copy.23 = bf16[256,256]{1,0:T(8,128)(2,1)} copy(bf16[256,256]{1,0:T(8,128)(2,1)} %get-tuple-element.14) | data formatting | bytes 262144
where the time goes:
time: 134 us; the launch traced here: 133 us
  Pallas kernels  125 us (93%)
  local copies, waits for them, and re-layouts  8.23 us (6%)
    pallas_call x1, Pallas kernels, on_device(): pl.pallas_call(functools.partial(kernel, G, R, C), out_shape=(tall, small...  125 us
    unnamed x5, local copies, waits for them, and re-layouts  8.23 us

commit v1 on v0

v1 whole, which is shorter than its diff:
```python
import functools

import jax
import jax.numpy as jnp
from jax import lax
from jax.experimental import pallas as pl
from jax.experimental.pallas import tpu as pltpu
from jax.sharding import PartitionSpec as P

B = 256
MESH = pl.DeviceIdType.MESH
BF = jnp.bfloat16
F32 = jnp.float32


def tdot(a, b):
    return lax.dot_general(a, b, (((0,), (0,)), ((), ())), preferred_element_type=F32)


def land(*conds):
    out = conds[0]
    for k in conds[1:]:
        out = jnp.logical_and(out, k)
    return out


def kernel(
    G, R, C,
    a_in, lu_in, mu_ref, du_in, ll_in, ml_ref, par_ref, lp_in, dl_in,
    x_out, diagu_out, y_out, yp_out, diagl_out,
    a_ref, lu_ref, ll_ref, du_ref, dl_ref, lp_ref,
    x_ref, y_ref, ybuf, zbuf, col, acc, part, near_y, near_x, sent_y, sent_x, last_y, last_x,
    rhs, lum, llm, xrow, selbuf, chy, chosen, part3, red, dufull, dpar, ypfull, back, dlfull,
    linked, terms, in_s, out_s,
    h_ss, h_rs, t_ss, t_rs, c_rs, v_ss, r_ss, x_ss,
    ny_ss, ny_rs, nx_ss, nx_rs, ly_ss, ly_rs, lx_ss, lx_rs,
    xr_ss, xr_rs, ch_ss, ch_rs,
    red_ss, red_rs, s_ss, s_rs,
):
    g, z, c = lax.axis_index("grp"), lax.axis_index("row"), lax.axis_index("col")
    n = G * R
    q = n // C
    CX = C // G
    y, x = lax.div(c, CX), lax.rem(c, CX)
    r = g * R + z
    h = lu_ref.shape[0]
    hb = W = h // B
    S = B // n
    H2 = h // 2
    panels = (lu_ref, ll_ref)
    masks = (mu_ref, ml_ref)
    primary = y == g
    zh = lax.div(z, q)
    home = zh == x
    oy = 1 - y

    def rdev(i):
        return (lax.div(i, R), lax.rem(i, R), c)

    def pdev(yy, xx):
        return (g, z, yy * CX + xx)

    def xo(o):
        return lax.rem(x + o, CX)

    def copy(src, dst, ss, rs, dev):
        return pltpu.make_async_remote_copy(
            src_ref=src, dst_ref=dst, send_sem=ss, recv_sem=rs, device_id=dev, device_id_type=MESH
        )

    ins = [
        pltpu.make_async_copy(src, dst, in_s.at[i])
        for i, (src, dst) in enumerate(
            ((lu_in, lu_ref), (ll_in, ll_ref), (a_in, a_ref), (lp_in, lp_ref), (du_in, du_ref), (dl_in, dl_ref))
        )
    ]
    barrier = pltpu.get_barrier_semaphore()
    for o in range(1, n):
        pl.semaphore_signal(barrier, inc=1, device_id=rdev(lax.rem(r + o, n)), device_id_type=MESH)
    for o in range(1, C):
        pl.semaphore_signal(
            barrier, inc=1, device_id=(g, z, lax.rem(c + o, C)), device_id_type=MESH
        )
    for i in ins:
        i.start()
    ins[0].wait()
    ins[1].wait()
    with jax.named_scope("barrier"):
        pl.semaphore_wait(barrier, n - 1 + C - 1)

    log = []

    def cut(w):
        return pl.ds(w * B, B)

    edge = (z < R - 1, z > 0)
    away = jnp.logical_not(home)
    outer = jnp.logical_or(z == 0, z == R - 1)
    far = ((zh + 1) * q < R, zh > 0)
    zj = lax.rem(z, q)

    def side_dev(side):
        return (g, z + 1 if side == 0 else z - 1, c)

    def col_u(o, l):
        return (y if l == 0 else oy) * CX + xo(o)

    def hop_copy(p, w):
        return copy(
            panels[p].at[cut(w), :], ybuf.at[p, cut(w), :], h_ss.at[p], h_rs.at[p, w],
            (g, z, g * CX + x),
        )

    def own_src(p, l, w):
        return panels[p].at[cut(w), :] if l == 0 else ybuf.at[p, cut(w), :]

    def at_col(p, j, u, w):
        return col.at[p, j * C + u, cut(w), :]

    def along(p, j, u, side, w, src):
        return ("v", p, side), lambda: copy(
            src, at_col(p, j, u, w), v_ss.at[p, side], c_rs.at[p, j * C + u, w], side_dev(side)
        )

    def relay(p, j, u, w, src):
        return None, lambda: copy(
            src, at_col(p, j, u, w), r_ss.at[p], c_rs.at[p, j * C + u, w], (1 - g, z, c)
        )

    def cross(p, z0, l, w, src):
        u, j = col_u(0, l), lax.rem(z0, q)
        return ("x", p, 0), lambda: copy(
            src, at_col(p, j, u, w), x_ss.at[p, 0], c_rs.at[p, j * C + u, w],
            pdev(y, lax.div(z0, q)),
        )

    def through(p, z0, side, w, src):
        return ("t", p, side), lambda: copy(
            src, zbuf.at[p, z0, cut(w), :], t_ss.at[p, side], t_rs.at[p, z0, w], side_dev(side)
        )

    def own_home(p, l, w, where):
        u, src = col_u(0, l), own_src(p, l, w)
        live = {"all": home, "outer": land(home, outer), "inner": land(home, z > 0, z < R - 1)}[where]
        outs = [(edge[side], along(p, zj, u, side, w, src)) for side in range(2)]
        outs.append((None, relay(p, zj, u, w, src)))

        def local():
            k = pltpu.make_async_copy(src, at_col(p, zj, u, w), c_rs.at[p, zj * C + u, w])
            k.start()
            k.wait()

        return live, (lambda: hop_copy(p, w)) if l == 1 else None, outs, local

    def own_away(p, l, w):
        src = own_src(p, l, w)
        outs = [(None, cross(p, z, l, w, src))]
        if l == 0:
            outs += [(far[side], through(p, z, side, w, src)) for side in range(2)]
        return away, (lambda: hop_copy(p, w)) if l == 1 else None, outs, None

    def transit(p, s, side, w):
        z0 = z - s if side == 0 else z + s
        b0 = lax.div(z0, q)
        ok = z0 >= 0 if side == 0 else z0 < R
        path = (b0 + 1) * q < R if side == 0 else b0 > 0
        at = zbuf.at[p, z0, cut(w), :]
        outs = [(edge[side], through(p, z0, side, w, at)), (zh != b0, cross(p, z0, 0, w, at))]
        return land(ok, path, b0 != x), through(p, z0, side, w, at)[1], outs, None

    def arrive(p, kind, i, o, l, w):
        j = lax.rem(zj + i, q) if kind == "home" else jnp.where(z < x * q, i, q - 1 - i)
        z0 = x * q + j
        u = col_u(o, l)
        up = land(z0 <= z, edge[0])
        down = land(z0 >= z, edge[1])
        outs = []
        at = at_col(p, j, u, w)
        if o != 0 and l == 0:
            up = land(up, lax.div(z + 1, q) == x)
            down = land(down, lax.div(z - 1 + q, q) == x + 1)
        if kind == "home" or o == 0 or l == 1:
            outs = [(up, along(p, j, u, 0, w, at)), (down, along(p, j, u, 1, w, at))]
        outs.append((None, relay(p, j, u, w, at)))
        return home if kind == "home" else away, relay(p, j, u, w, at)[1], outs, None

    def emit(f, *args):
        log.append((f, args))
        live, first, outs, local = f(*args)

        def body():
            if first is not None:
                first().wait_recv()
            for cond, (_, make) in outs:
                if cond is None:
                    make().start()
                else:
                    pl.when(cond)(lambda: make().start())
            if local is not None:
                local()

        pl.when(live)(body)

    def wait_blocks(sem, p, k):
        at = col.at[p, pl.ds(0, k)]
        copy(at, at, sem, sem, rdev(r)).wait_send()

    def wait_sends():
        for p in range(2):
            wait_blocks(r_ss.at[p], p, q * C)
        count = {}
        for f, args in dict.fromkeys(log):
            if args[-1] == 0 or (f is own_home and args[-2] == 0):
                live, _, outs, _ = f(*args)
                for cond, (key, _) in outs:
                    if key is not None:
                        on = live if cond is None else land(live, cond)
                        count[key] = count.get(key, 0) + jnp.where(on, 1, 0)
        for (kind, p, side), number in sorted(count.items()):
            sem = {"v": v_ss, "x": x_ss, "t": t_ss}[kind].at[p, side]
            for k in range(1, {"v": q * C, "x": R + G, "t": R}[kind] + 1):
                pl.when(number == k)(lambda: wait_blocks(sem, p, k))

    chunks = range(W)
    others = range(1, CX)
    rest = range(1, q)
    TAU, HOP = 1.4, 3.0

    def at_home():
        ev = []

        def add(t, f, *args, slope=TAU):
            for w in chunks:
                ev.append((t + slope * w, f, (*args, w) if f is not own_home else (*args[:2], w, args[2])))

        add(0, own_home, 0, 0, "all", slope=0)
        for s in range(1, R):
            for side in range(2):
                add(HOP * s, transit, 0, s, side)
                add(4.4 + HOP * s, transit, 1, s, side)
        add(6.2, own_home, 0, 1, "all", slope=0)
        add(16.5, own_home, 1, 1, "outer", slope=0)
        add(16.7, own_home, 1, 0, "outer", slope=0)
        add(24, own_home, 1, 1, "inner", slope=0)
        add(28, own_home, 1, 0, "inner", slope=0)
        for o in others:
            add(3.1, arrive, 0, "home", 0, o, 0)
            add(8, arrive, 0, "home", 0, o, 1)
            add(19.2, arrive, 1, "home", 0, o, 0)
            add(16, arrive, 1, "home", 0, o, 1)
        for i in rest:
            add(3.05, arrive, 0, "home", i, 0, 0)
            add(11.5, arrive, 0, "home", i, 0, 1)
            add(25, arrive, 1, "home", i, 0, 1)
            add(29, arrive, 1, "home", i, 0, 0)
            for o in others:
                add(8.5, arrive, 0, "home", i, o, 0)
                add(15.7, arrive, 0, "home", i, o, 1)
                add(21, arrive, 1, "home", i, o, 1)
                add(28.5, arrive, 1, "home", i, o, 0)
        return ev

    def at_away():
        ev = []

        def add(t, f, *args, slope=TAU):
            for w in chunks:
                ev.append((t + slope * w, f, (*args, w)))

        add(0, own_away, 0, 0, slope=0)
        for s in range(1, R):
            for side in range(2):
                add(HOP * s, transit, 0, s, side)
                add(4.5 + HOP * s, transit, 1, s, side)
        add(3.2, own_away, 0, 1)
        add(6.1, own_away, 1, 0, slope=0)
        add(9, own_away, 1, 1, slope=0)
        for i in range(q):
            add(3.05 + 4.35 * i, arrive, 0, "away", i, 0, 0)
            add(11.5 + 8.4 * i, arrive, 0, "away", i, 0, 1)
            add(36.8 + 4.2 * i, arrive, 1, "away", i, 0, 1)
            add(45.2 + 4.2 * i, arrive, 1, "away", i, 0, 0)
            for o in others:
                add(9.2 + 3.1 * i, arrive, 0, "away", i, o, 0)
                add(15.7 + 8.4 * i, arrive, 0, "away", i, o, 1)
                add(23.6 + 3.9 * i, arrive, 1, "away", i, o, 0)
                add(28.3 + 4.2 * i, arrive, 1, "away", i, o, 1)
        return ev

    timed = (sorted(at_home(), key=lambda e: e[0]), sorted(at_away(), key=lambda e: e[0]))

    def events(home_to, away_to):
        for which, cond, to in ((0, home, home_to), (1, away, away_to)):
            now = [e for e in timed[which] if e[0] < to]
            timed[which][:] = timed[which][len(now):]
            if now:
                @pl.when(land(primary, cond))
                def _():
                    for _, f, args in now:
                        emit(f, *args)

    def kd(o, l):
        return l * CX + o

    def ny_copy(p, o):
        return copy(
            part.at[p, kd(o, 1), pl.ds(0, H2), :], near_y.at[p, o], ny_ss.at[p], ny_rs.at[p, o],
            pdev(oy, x),
        )

    def nx_copy(p, o, l):
        i = (CX - o) * G + l
        return copy(
            part.at[p, kd(o, l), pl.ds(H2, H2), :], near_x.at[p, i], nx_ss.at[p], nx_rs.at[p, i],
            pdev(y, xo(o)),
        )

    def ly_copy(p, o):
        return copy(
            sent_y.at[p, o], last_y.at[p, CX - o], ly_ss.at[p], ly_rs.at[p, CX - o],
            pdev(y, xo(o)),
        )

    def lx_copy(p):
        return copy(sent_x.at[p], last_x.at[p], lx_ss.at[p], lx_rs.at[p], pdev(oy, x))

    def product(p, o, l):
        u = (y if l == 0 else oy) * CX + xo(o)
        k = kd(o, l)

        @pl.when(jnp.logical_not(primary))
        def _():
            for j in range(q):
                for w in range(W):
                    relay(p, j, u, w, at_col(p, j, u, w))[1]().wait_recv()

        @pl.loop(0, q * hb)
        def _(i):
            j, t = lax.div(i, hb), lax.rem(i, hb)
            keep = masks[p][u, c * q * hb + i] > 0
            rows = pl.ds(pl.multiple_of(t * B, B), B)
            blk = col[p, j * C + u, rows, :]
            rhs[pl.ds(pl.multiple_of(i * B, B), B), :] = jnp.where(keep, blk, jnp.zeros_like(blk))

        @pl.loop(0, 2)
        def _(t):
            rows = pl.ds(pl.multiple_of(t * H2, H2), H2)
            v = jnp.dot(a_ref[rows, :], rhs[...], preferred_element_type=F32)
            acc[p, k, rows, :] = v
            part[p, k, rows, :] = v.astype(BF)

        if l == 1:
            ny_copy(p, o).start()
        if o != 0:
            nx_copy(p, o, l).start()

    top, low = pl.ds(0, H2), pl.ds(H2, H2)

    def second(p):
        for o in range(1, CX):
            ny_copy(p, o).wait_recv()
            sent_y[p, o] = (acc[p, kd(o, 0), top, :] + near_y[p, o].astype(F32)).astype(BF)
            ly_copy(p, o).start()
        v = acc[p, kd(0, 1), low, :]
        for o in range(1, CX):
            nx_copy(p, CX - o, 1).wait_recv()
            v = v + near_x[p, o * G + 1].astype(F32)
        sent_x[p] = v.astype(BF)
        lx_copy(p).start()

    def total(p):
        ny_copy(p, 0).wait_recv()
        v = acc[p, 0, top, :] + near_y[p, 0].astype(F32)
        for o in range(1, CX):
            ly_copy(p, CX - o).wait_recv()
            v = v + last_y[p, o].astype(F32)
        w = acc[p, 0, low, :]
        for o in range(1, CX):
            nx_copy(p, CX - o, 0).wait_recv()
            w = w + near_x[p, o * G].astype(F32)
        lx_copy(p).wait_recv()
        w = w + last_x[p].astype(F32)
        return (-v).astype(BF), (-w).astype(BF)

    def red_copy(k, o):
        i = lax.rem(r + o, n)
        return copy(
            part3.at[k, pl.ds(pl.multiple_of(i * S, S), S), :], red.at[k, r],
            red_ss.at[k], red_rs.at[k], rdev(i),
        )

    def send_sum(k):
        red[k, r] = part3[k, pl.ds(pl.multiple_of(r * S, S), S), :]
        for o in range(1, n):
            red_copy(k, o).start()

    def all_red(k):
        at = red.at[k, pl.ds(0, n - 1)]
        return copy(at, at, red_ss.at[k], red_rs.at[k], rdev(r))

    def take_sum(k):
        all_red(k).wait_recv()
        v = red[k, 0].astype(F32)
        for i in range(1, n):
            v = v + red[k, i].astype(F32)
        return v

    mine = pl.ds(pl.multiple_of(r * S, S), S)

    def spread(i, buf):
        for o in range(1, n):
            copy(
                buf.at[mine, :], buf.at[mine, :], s_ss.at[i], s_rs.at[i], rdev(lax.rem(r + o, n))
            ).start()

    def all_spread(i, buf):
        at = buf.at[pl.ds(0, (n - 1) * S), :]
        return copy(at, at, s_ss.at[i], s_rs.at[i], rdev(r))

    def dp_copy(o):
        return copy(
            dpar.at[c], dpar.at[c], s_ss.at[3], s_rs.at[3], (g, z, lax.rem(c + o, C))
        )

    def all_dp():
        at = dpar.at[pl.ds(0, C - 1)]
        return copy(at, at, s_ss.at[3], s_rs.at[3], rdev(r))

    def xr_copy(o, w):
        return copy(
            x_ref.at[cut(w), :], xrow.at[CX - o, cut(w), :], xr_ss.at[0],
            xr_rs.at[CX - o, w], pdev(y, xo(o)),
        )

    def ch_copy(w):
        return copy(selbuf.at[cut(w), :], chy.at[cut(w), :], ch_ss.at[0], ch_rs.at[w], pdev(oy, x))

    def pick(who, base, w):
        v = base
        for o in range(CX):
            src = x_ref if o == 0 else xrow.at[o]
            v = jnp.where(who == y * CX + xo(o), src[cut(w), :], v)
        return v

    def out_copy(i, src, dst):
        return pltpu.make_async_copy(src, dst, out_s.at[i])

    def step(name, f, cond=None):
        with jax.named_scope(name):
            if cond is None:
                f()
            else:
                pl.when(cond)(f)

    def start_hops():
        for p in range(2):
            for w in range(W):
                hop_copy(p, w).start()

    def mask_own():
        @pl.loop(0, hb)
        def _(t):
            rows = pl.ds(pl.multiple_of(t * B, B), B)
            ub, lb = lu_ref[rows, :], ll_ref[rows, :]
            lum[rows, :] = jnp.where(mu_ref[c, r * hb + t] > 0, ub, jnp.zeros_like(ub))
            llm[rows, :] = jnp.where(ml_ref[c, r * hb + t] > 0, lb, jnp.zeros_like(lb))

    def x_final():
        xt, xl = total(0)
        x_ref[top, :] = xt
        x_ref[low, :] = xl
        for w in range(W):
            for o in range(1, CX):
                xr_copy(o, w).start()
        out_copy(0, x_ref, x_out).start()
        part3[0] = tdot(lum[...], x_ref[...]).astype(BF)
        send_sum(0)

    def choose_send():
        to = par_ref[oy * CX + x]
        for w in range(W):
            for o in range(1, CX):
                xr_copy(CX - o, w).wait_recv()
            selbuf[cut(w), :] = pick(to, x_ref[cut(w), :], w)
            ch_copy(w).start()

    def diag_upper():
        dslice = (du_ref[mine, :] - take_sum(0)).astype(BF)
        dufull[mine, :] = dslice
        dpar[c] = dslice
        for o in range(1, C):
            dp_copy(o).start()
        spread(0, dufull)

    here = par_ref[c]

    def choose_take():
        for w in range(W):
            ch_copy(w).wait_recv()
            chosen[cut(w), :] = pick(here, chy[cut(w), :], w)

    def crossed():
        part3[1] = tdot(chosen[...], llm[...]).astype(BF)
        send_sum(1)

    def coupling():
        @pl.loop(0, hb)
        def _(t):
            rows = pl.ds(pl.multiple_of(t * B, B), B)
            v = jnp.dot(chosen[rows, :], lp_ref[...], preferred_element_type=F32)
            acc[1, 0, rows, :] += v
            linked[rows, :] = v.astype(BF)

    def parent_terms():
        all_dp().wait_recv()
        v = jnp.dot(dpar[here], lp_ref[...], preferred_element_type=F32)
        terms[...] = v
        back[...] = -tdot(linked[...], llm[...]) - tdot(lp_ref[mine, :], v.astype(BF))

    def y_final():
        yt, yl = total(1)
        y_ref[top, :] = yt
        y_ref[low, :] = yl
        part3[2] = (tdot(llm[...], y_ref[...]) + back[...]).astype(BF)
        send_sum(2)
        out_copy(1, y_ref, y_out).start()

    def y_parent():
        ypfull[mine, :] = (-(take_sum(1) + terms[...])).astype(BF)
        spread(1, ypfull)

    def diag_lower():
        dlfull[mine, :] = (dl_ref[mine, :] - take_sum(2)).astype(BF)
        spread(2, dlfull)

    def gather_upper():
        all_spread(0, dufull).wait_recv()
        out_copy(2, dufull, diagu_out).start()

    def gather_parent():
        all_spread(1, ypfull).wait_recv()
        out_copy(3, ypfull, yp_out).start()

    def gather_lower():
        all_spread(2, dlfull).wait_recv()
        out_copy(4, dlfull, diagl_out).start()

    def wait_ins():
        for i in ins[2:]:
            i.wait()

    def products(p, l):
        for o in range(1, CX):
            product(p, o, l)

    pl.when(jnp.logical_not(primary))(start_hops)
    step("ev0", lambda: events(0.1, 0.1))
    step("mask", mask_own)
    step("ev1", lambda: events(11.9, 10.9))
    wait_ins()
    step("prod_u1", lambda: product(0, 0, 0))
    step("ev2", lambda: events(13.5, 16.0))
    step("prod_u4", lambda: products(0, 0))
    step("ev3", lambda: events(15.6, 23.5))
    step("prod_u2", lambda: product(0, 0, 1))
    step("ev4", lambda: events(20.2, 27.2))
    step("prod_u3", lambda: products(0, 1))
    step("ev5", lambda: events(99, 36.5))
    step("lprod_u3", lambda: products(1, 1))
    step("lprod_u4", lambda: products(1, 0))
    step("second", lambda: second(0))
    step("ev6", lambda: events(99, 44.5))
    step("lprod_u2", lambda: product(1, 0, 1))
    step("x_final", x_final)
    step("second_l", lambda: second(1))
    step("ev7", lambda: events(99, 48.5))
    step("choose_send", choose_send)
    step("diag_upper", diag_upper)
    step("ev8", lambda: events(99, 99))
    step("lprod_u1", lambda: product(1, 0, 0))
    step("choose_take", choose_take)
    step("crossed", crossed)
    step("coupling", coupling)
    step("parent_terms", parent_terms)
    step("y_final", y_final)
    step("y_parent", y_parent)
    step("diag_lower", diag_lower)
    step("gather_upper", gather_upper)
    step("gather_parent", gather_parent)
    step("gather_lower", gather_lower)

    def finish():
        @pl.when(primary)
        def _():
            wait_sends()

        @pl.when(jnp.logical_not(primary))
        def _():
            for p in range(2):
                copy(ybuf.at[p], ybuf.at[p], h_ss.at[p], h_ss.at[p], rdev(r)).wait_send()

        def sent(sem, at):
            copy(at, at, sem, sem, rdev(r)).wait_send()

        for p in range(2):
            sent(ny_ss.at[p], near_y.at[p])
            sent(nx_ss.at[p], near_x.at[p, pl.ds(0, (CX - 1) * G)])
            sent(ly_ss.at[p], last_y.at[p, pl.ds(0, CX - 1)])
            sent(lx_ss.at[p], last_x.at[p])
        sent(xr_ss.at[0], xrow.at[pl.ds(0, CX - 1)])
        sent(ch_ss.at[0], chy)
        for k in range(3):
            all_red(k).wait_send()
        for i, buf in enumerate((dufull, ypfull, dlfull)):
            all_spread(i, buf).wait_send()
        all_dp().wait_send()
        for i, (src, dst) in enumerate(
            ((x_ref, x_out), (y_ref, y_out), (dufull, diagu_out), (ypfull, yp_out), (dlfull, diagl_out))
        ):
            out_copy(i, src, dst).wait()

    step("finish", finish)


def on_device(G, R, C, a, lu, mu, du, ll, ml, par, lp, dl):
    h = lu.shape[0]
    n = G * R
    q = n // C
    S = B // n
    CX = C // G
    W = h // B
    H2 = h // 2
    hbm = pl.BlockSpec(memory_space=pl.ANY)
    sm = pl.BlockSpec(memory_space=pltpu.SMEM)
    dma = pltpu.SemaphoreType.DMA
    small = jax.ShapeDtypeStruct((B, B), BF)
    tall = jax.ShapeDtypeStruct((h, B), BF)
    vm = pltpu.VMEM
    return pl.pallas_call(
        functools.partial(kernel, G, R, C),
        out_shape=(tall, small, tall, small, small),
        in_specs=[hbm, hbm, sm, hbm, hbm, sm, sm, hbm, hbm],
        out_specs=(hbm,) * 5,
        scratch_shapes=[
            vm(a.shape, BF), vm((h, B), BF), vm((h, B), BF), vm((B, B), F32), vm((B, B), F32), vm((B, B), BF),
            vm((h, B), BF), vm((h, B), BF),
            vm((2, h, B), BF),
            vm((2, R, h, B), BF),
            vm((2, q * C, h, B), BF),
            vm((2, C, h, B), F32),
            vm((2, C, h, B), BF),
            vm((2, CX, H2, B), BF),
            vm((2, CX * G, H2, B), BF),
            vm((2, CX, H2, B), BF),
            vm((2, H2, B), BF),
            vm((2, CX, H2, B), BF),
            vm((2, H2, B), BF),
            vm((q * h, B), BF),
            vm((h, B), BF), vm((h, B), BF),
            vm((CX, h, B), BF), vm((h, B), BF), vm((h, B), BF), vm((h, B), BF),
            vm((3, B, B), BF),
            vm((3, n, S, B), BF),
            vm((B, B), BF),
            vm((C, S, B), BF),
            vm((B, B), BF),
            vm((B, B), F32),
            vm((B, B), BF),
            vm((h, B), BF), vm((S, B), F32),
            dma((6,)), dma((5,)),
            dma((2,)), dma((2, W)), dma((2, 2)), dma((2, R, W)),
            dma((2, q * C, W)), dma((2, 2)), dma((2,)), dma((2, 1)),
            dma((2,)), dma((2, CX)), dma((2,)), dma((2, CX * G)),
            dma((2,)), dma((2, CX)), dma((2,)), dma((2,)),
            dma((1,)), dma((CX, W)), dma((1,)), dma((W,)),
            dma((3,)), dma((3,)), dma((4,)), dma((4,)),
        ],
        compiler_params=pltpu.CompilerParams(
            collective_id=0, has_side_effects=True, vmem_limit_bytes=60 * 1024 * 1024
        ),
    )(a, lu, mu, du, ll, ml, par, lp, dl)


def solution(mesh):
    tall, wide = P(("grp", "row"), "col"), P(None, "col")
    return jax.shard_map(
        functools.partial(
            on_device, mesh.shape["grp"], mesh.shape["row"], mesh.shape["col"]
        ),
        mesh=mesh,
        in_specs=(tall, tall, P(), wide, tall, P(), P(), wide, wide),
        out_specs=(tall, wide, tall, wide, wide),
        check_vma=False,
    )
```

time: 134 us -> 124 us (0.925)
  Pallas kernels: 125 us -> 114 us
    pallas_call x1, Pallas kernels: 125 us -> 114 us  [on_device(): pl.pallas_call(functools.partial(kernel, G, R, C), out_shape=(tall, small...]
where the time goes in v1:
time: 124 us; the launch traced here: 123 us
  Pallas kernels  114 us (92%)
  local copies, waits for them, and re-layouts  8.23 us (7%)
    pallas_call x1, Pallas kernels, on_device(): pl.pallas_call(functools.partial(kernel, G, R, C), out_shape=(tall, small...  114 us
    unnamed x5, local copies, waits for them, and re-layouts  8.23 us

profile of v1, /device:TPU:0, one launch (start us, length us, event | category | flops | bytes accessed | tf_op | source)
XLA Modules:
  0.0 123.2 jit_solution(7188118378156339085)
XLA Ops:
  0.6 114.4 %shard_map.128 = (bf16[768,256]{1,0:T(8,128)(2,1)}, bf16[256,256]{1,0:T(8,128)(2,1)}, bf16[768,256]{1,0:T(8,128)(2,1)}, bf16[256,256]{1,0:T(8,128)(2,1)}, bf16[256,256]{1,0:T(8,128)(2,1)}) custom-call(bf16[768,1536]{1,0:T(8,128)(2,1)} %a_in.1, bf16[768,256]{1,0:T(8,128)(2,1)} %lu_in.1, s32[4,24]{1,0:T(4,128)} %mu_ref.1, f32[256,256]{1,0:T(8,128)} %du_in.1, ...), custom_call_target="tpu_custom_call" | custom-call | tf_op jit(solution)/shard_map/pallas_call | solution.py:639
  115.0 1.8 %copy.19 = bf16[768,256]{1,0:T(8,128)(2,1)} copy(bf16[768,256]{1,0:T(8,128)(2,1)} %get-tuple-element.10) | data formatting | bytes 786432
  116.8 1.6 %copy.20 = bf16[256,256]{1,0:T(8,128)(2,1)} copy(bf16[256,256]{1,0:T(8,128)(2,1)} %get-tuple-element.11) | data formatting | bytes 262144
  118.3 1.8 %copy.21 = bf16[768,256]{1,0:T(8,128)(2,1)} copy(bf16[768,256]{1,0:T(8,128)(2,1)} %get-tuple-element.12) | data formatting | bytes 786432
  120.1 1.6 %copy.22 = bf16[256,256]{1,0:T(8,128)(2,1)} copy(bf16[256,256]{1,0:T(8,128)(2,1)} %get-tuple-element.13) | data formatting | bytes 262144
  121.7 1.6 %copy.23 = bf16[256,256]{1,0:T(8,128)(2,1)} copy(bf16[256,256]{1,0:T(8,128)(2,1)} %get-tuple-element.14) | data formatting | bytes 262144

commit v2 on v1

--- a/solution.py
+++ b/solution.py
@@ -22,6 +22,117 @@
     for k in conds[1:]:
         out = jnp.logical_and(out, k)
     return out
+
+
+TAU = 1.4
+
+
+def plan(kind, R, q, CX, W):
+    ev = []
+
+    def add(t, name, *args, slope=TAU):
+        for w in range(W):
+            ev.append((t + slope * w, name, args, w))
+
+    def at(t, name, *args):
+        add(t, name, *args, slope=0.001)
+
+    others = range(1, CX)
+    inner = kind[1] == "I"
+    if CX != 2:
+        for p, l in ((0, 0), (0, 1), (1, 0), (1, 1)):
+            if kind[0] == "H":
+                for part in ("far", "near"):
+                    at(0, "own", p, l, part)
+            else:
+                at(0, "away", p, l)
+        for p in range(2):
+            for s in range(1, R):
+                for side in range(2):
+                    at(1 + p + s / R, "transit", p, s, side)
+            t = (5, 33)[p]
+            if kind[0] == "H":
+                for part in ("far", "near"):
+                    for o in others:
+                        for l in range(2):
+                            at(t, "arrive", p, "home", 0, o, l, part)
+            for l in range(2):
+                for o in range(CX):
+                    for i in range(0 if kind[0] == "A" else 1, q):
+                        at(t + 1 + l + 0.1 * o, "arrive", p, ("away" if kind[0] == "A" else "home"), i, o, l, "far")
+        return sorted(ev, key=lambda e: e[0])
+    if kind[0] == "H":
+        at(0, "own", 0, 0, "far")
+        for s in range(1, R):
+            for side in range(2):
+                add((0 if inner else 0.1) + 3.9 * s, "transit", 0, s, side)
+                add(9.1 + 4 * s if inner else 25.2 + 4.1 * s, "transit", 1, s, side)
+        if inner:
+            at(7, "own", 0, 1, "far")
+            at(12.2, "own", 0, 0, "near")
+            at(12.6, "own", 0, 1, "near")
+            at(24.8, "own", 1, 1, "far")
+            at(28.7, "own", 1, 0, "far")
+            at(28.8, "own", 1, 1, "near")
+            at(28.9, "own", 1, 0, "near")
+        else:
+            at(0.1, "own", 0, 0, "near")
+            add(4.0, "own", 0, 1, "far")
+            add(4.01, "own", 0, 1, "near")
+            at(18.2, "own", 1, 1, "far")
+            at(18.3, "own", 1, 1, "near")
+            at(18.4, "own", 1, 0, "far")
+            at(18.5, "own", 1, 0, "near")
+        for o in others:
+            add(4.05, "arrive", 0, "home", 0, o, 0, "far")
+            add(8.0, "arrive", 0, "home", 0, o, 1, "far")
+            if inner:
+                at(12.4, "arrive", 0, "home", 0, o, 0, "near")
+                at(12.8, "arrive", 0, "home", 0, o, 1, "near")
+                at(17, "arrive", 1, "home", 0, o, 1, "far")
+                at(19.9, "arrive", 1, "home", 0, o, 0, "far")
+                at(25, "arrive", 1, "home", 0, o, 1, "near")
+                at(25.1, "arrive", 1, "home", 0, o, 0, "near")
+            else:
+                add(8.01, "arrive", 0, "home", 0, o, 1, "near")
+                at(11.5, "arrive", 0, "home", 0, o, 0, "near")
+                add(15.2, "arrive", 1, "home", 0, o, 1, "far")
+                add(15.21, "arrive", 1, "home", 0, o, 1, "near")
+                at(20.2, "arrive", 1, "home", 0, o, 0, "far")
+                at(20.3, "arrive", 1, "home", 0, o, 0, "near")
+        for i in range(1, q):
+            first = (4.02, 9.0, 12.5, 16.5) if inner else (16.5, 25.0, 29.2, 20.8)
+            last = (29.2, 25.0, 20.7, 33.5) if inner else (54.3, 50.1, 41.6, 45.8)
+            for p, (t1, t2, t3, t4) in ((0, first), (1, last)):
+                add(t1, "arrive", p, "home", i, 0, 0, "far")
+                add(t2, "arrive", p, "home", i, 0, 1, "far")
+                for o in others:
+                    add(t3, "arrive", p, "home", i, o, 1, "far")
+                    add(t4, "arrive", p, "home", i, o, 0, "far")
+    else:
+        at(0, "away", 0, 0)
+        for s in range(1, R):
+            for side in range(2):
+                add(0.1 + 3.9 * s, "transit", 0, s, side)
+                add(11.5 + 3.9 * s, "transit", 1, s, side)
+        add(4.1, "away", 0, 1)
+        add(8.5, "away", 1, 1)
+        at(11.6, "away", 1, 0)
+        d = 0 if inner else 3.9
+        for i in range(q):
+            add(4.05 + d + 3.95 * i, "arrive", 0, "away", i, 0, 0, "far")
+            add(12.1 + d + 8.5 * i, "arrive", 0, "away", i, 0, 1, "far")
+            add(37.5 + d + 4.2 * i, "arrive", 1, "away", i, 0, 1, "far")
+            add(46 + d + 4.2 * i, "arrive", 1, "away", i, 0, 0, "far")
+            for o in others:
+                add(8.2 + d + 4 * i, "arrive", 0, "away", i, o, 0, "far")
+                add(16.4 + d + 8.4 * i, "arrive", 0, "away", i, o, 1, "far")
+                if inner:
+                    at(27.9 + 0.1 * i, "arrive", 1, "away", i, o, 0, "far")
+                else:
+                    add(37.2 + 4.2 * i, "arrive", 1, "away", i, o, 0, "far")
+                add(29 + d + 4.2 * i, "arrive", 1, "away", i, o, 1, "far")
+    return sorted(ev, key=lambda e: e[0])
 
 
 def kernel(
@@ -139,20 +250,32 @@
             src, zbuf.at[p, z0, cut(w), :], t_ss.at[p, side], t_rs.at[p, z0, w], side_dev(side)
         )
 
-    def own_home(p, l, w, where):
+    near_side = (lax.div(z + 1, q) == x, lax.div(z - 1 + q, q) == x + 1)
+
+    def own(p, l, part, w):
         u, src = col_u(0, l), own_src(p, l, w)
-        live = {"all": home, "outer": land(home, outer), "inner": land(home, z > 0, z < R - 1)}[where]
-        outs = [(edge[side], along(p, zj, u, side, w, src)) for side in range(2)]
-        outs.append((None, relay(p, zj, u, w, src)))
+
+        def sides(near):
+            return [
+                (
+                    land(edge[k], near_side[k] if near else jnp.logical_not(near_side[k])),
+                    along(p, zj, u, k, w, src),
+                )
+                for k in range(2)
+            ]
+
+        if part == "near":
+            return home, None, sides(True), None
 
         def local():
             k = pltpu.make_async_copy(src, at_col(p, zj, u, w), c_rs.at[p, zj * C + u, w])
             k.start()
             k.wait()
 
-        return live, (lambda: hop_copy(p, w)) if l == 1 else None, outs, local
-
-    def own_away(p, l, w):
+        outs = sides(False) + [(None, relay(p, zj, u, w, src))]
+        return home, (lambda: hop_copy(p, w)) if l == 1 else None, outs, local
+
+    def away_own(p, l, w):
         src = own_src(p, l, w)
         outs = [(None, cross(p, z, l, w, src))]
         if l == 0:
@@ -168,21 +291,31 @@
         outs = [(edge[side], through(p, z0, side, w, at)), (zh != b0, cross(p, z0, 0, w, at))]
         return land(ok, path, b0 != x), through(p, z0, side, w, at)[1], outs, None
 
-    def arrive(p, kind, i, o, l, w):
+    def arrive(p, kind, i, o, l, part, w):
         j = lax.rem(zj + i, q) if kind == "home" else jnp.where(z < x * q, i, q - 1 - i)
         z0 = x * q + j
         u = col_u(o, l)
-        up = land(z0 <= z, edge[0])
-        down = land(z0 >= z, edge[1])
+        at = at_col(p, j, u, w)
+        side = (land(z0 <= z, edge[0]), land(z0 >= z, edge[1]))
+        late = o != 0 and l == 0
         outs = []
-        at = at_col(p, j, u, w)
-        if o != 0 and l == 0:
-            up = land(up, lax.div(z + 1, q) == x)
-            down = land(down, lax.div(z - 1 + q, q) == x + 1)
-        if kind == "home" or o == 0 or l == 1:
-            outs = [(up, along(p, j, u, 0, w, at)), (down, along(p, j, u, 1, w, at))]
+        for k in range(2):
+            step_to = along(p, j, u, k, w, at)
+            if kind == "away":
+                if not late:
+                    outs.append((side[k], step_to))
+            elif i == 0:
+                if part == "near":
+                    outs.append((land(side[k], near_side[k]), step_to))
+                elif not late:
+                    outs.append((land(side[k], jnp.logical_not(near_side[k])), step_to))
+            else:
+                outs.append((land(side[k], near_side[k]) if late else side[k], step_to))
+        live = home if kind == "home" else away
+        if part == "near":
+            return live, None, outs, None
         outs.append((None, relay(p, j, u, w, at)))
-        return home if kind == "home" else away, relay(p, j, u, w, at)[1], outs, None
+        return live, relay(p, j, u, w, at)[1], outs, None
 
     def emit(f, *args):
         log.append((f, args))
@@ -210,7 +343,7 @@
             wait_blocks(r_ss.at[p], p, q * C)
         count = {}
         for f, args in dict.fromkeys(log):
-            if args[-1] == 0 or (f is own_home and args[-2] == 0):
+            if args[-1] == 0:
                 live, _, outs, _ = f(*args)
                 for cond, (key, _) in outs:
                     if key is not None:
@@ -221,83 +354,23 @@
             for k in range(1, {"v": q * C, "x": R + G, "t": R}[kind] + 1):
                 pl.when(number == k)(lambda: wait_blocks(sem, p, k))
 
-    chunks = range(W)
-    others = range(1, CX)
-    rest = range(1, q)
-    TAU, HOP = 1.4, 3.0
-
-    def at_home():
-        ev = []
-
-        def add(t, f, *args, slope=TAU):
-            for w in chunks:
-                ev.append((t + slope * w, f, (*args, w) if f is not own_home else (*args[:2], w, args[2])))
-
-        add(0, own_home, 0, 0, "all", slope=0)
-        for s in range(1, R):
-            for side in range(2):
-                add(HOP * s, transit, 0, s, side)
-                add(4.4 + HOP * s, transit, 1, s, side)
-        add(6.2, own_home, 0, 1, "all", slope=0)
-        add(16.5, own_home, 1, 1, "outer", slope=0)
-        add(16.7, own_home, 1, 0, "outer", slope=0)
-        add(24, own_home, 1, 1, "inner", slope=0)
-        add(28, own_home, 1, 0, "inner", slope=0)
-        for o in others:
-            add(3.1, arrive, 0, "home", 0, o, 0)
-            add(8, arrive, 0, "home", 0, o, 1)
-            add(19.2, arrive, 1, "home", 0, o, 0)
-            add(16, arrive, 1, "home", 0, o, 1)
-        for i in rest:
-            add(3.05, arrive, 0, "home", i, 0, 0)
-            add(11.5, arrive, 0, "home", i, 0, 1)
-            add(25, arrive, 1, "home", i, 0, 1)
-            add(29, arrive, 1, "home", i, 0, 0)
-            for o in others:
-                add(8.5, arrive, 0, "home", i, o, 0)
-                add(15.7, arrive, 0, "home", i, o, 1)
-                add(21, arrive, 1, "home", i, o, 1)
-                add(28.5, arrive, 1, "home", i, o, 0)
-        return ev
-
-    def at_away():
-        ev = []
-
-        def add(t, f, *args, slope=TAU):
-            for w in chunks:
-                ev.append((t + slope * w, f, (*args, w)))
-
-        add(0, own_away, 0, 0, slope=0)
-        for s in range(1, R):
-            for side in range(2):
-                add(HOP * s, transit, 0, s, side)
-                add(4.5 + HOP * s, transit, 1, s, side)
-        add(3.2, own_away, 0, 1)
-        add(6.1, own_away, 1, 0, slope=0)
-        add(9, own_away, 1, 1, slope=0)
-        for i in range(q):
-            add(3.05 + 4.35 * i, arrive, 0, "away", i, 0, 0)
-            add(11.5 + 8.4 * i, arrive, 0, "away", i, 0, 1)
-            add(36.8 + 4.2 * i, arrive, 1, "away", i, 0, 1)
-            add(45.2 + 4.2 * i, arrive, 1, "away", i, 0, 0)
-            for o in others:
-                add(9.2 + 3.1 * i, arrive, 0, "away", i, o, 0)
-                add(15.7 + 8.4 * i, arrive, 0, "away", i, o, 1)
-                add(23.6 + 3.9 * i, arrive, 1, "away", i, o, 0)
-                add(28.3 + 4.2 * i, arrive, 1, "away", i, o, 1)
-        return ev
-
-    timed = (sorted(at_home(), key=lambda e: e[0]), sorted(at_away(), key=lambda e: e[0]))
-
-    def events(home_to, away_to):
-        for which, cond, to in ((0, home, home_to), (1, away, away_to)):
-            now = [e for e in timed[which] if e[0] < to]
-            timed[which][:] = timed[which][len(now):]
+    handlers = {"own": own, "away": away_own, "transit": transit, "arrive": arrive}
+    kinds = ("HI", "HO", "AI", "AO")
+    timed = {k: plan(k, R, q, CX, W) for k in kinds}
+    is_kind = {
+        "HI": land(home, jnp.logical_not(outer)), "HO": land(home, outer),
+        "AI": land(away, jnp.logical_not(outer)), "AO": land(away, outer),
+    }
+
+    def events(*until):
+        for k, to in zip(kinds, until):
+            now = [e for e in timed[k] if e[0] < to]
+            timed[k] = timed[k][len(now):]
             if now:
-                @pl.when(land(primary, cond))
+                @pl.when(land(primary, is_kind[k]))
                 def _():
-                    for _, f, args in now:
-                        emit(f, *args)
+                    for _, name, args, w in now:
+                        emit(handlers[name], *args, w)
 
     def kd(o, l):
         return l * CX + o
@@ -554,29 +627,32 @@
             product(p, o, l)
 
     pl.when(jnp.logical_not(primary))(start_hops)
-    step("ev0", lambda: events(0.1, 0.1))
+    late_home = is_kind["HO"]
+    step("ev0", lambda: events(0.1, 0.2, 0.1, 0.1))
     step("mask", mask_own)
-    step("ev1", lambda: events(11.9, 10.9))
+    step("ev1", lambda: events(11.9, 19.5, 10.9, 14.9))
     wait_ins()
     step("prod_u1", lambda: product(0, 0, 0))
-    step("ev2", lambda: events(13.5, 16.0))
+    step("ev2", lambda: events(19.5, 23.9, 15.1, 19.0))
     step("prod_u4", lambda: products(0, 0))
-    step("ev3", lambda: events(15.6, 23.5))
+    step("ev3", lambda: events(19.5, 28.0, 23.5, 27.4))
     step("prod_u2", lambda: product(0, 0, 1))
-    step("ev4", lambda: events(20.2, 27.2))
+    step("ev4", lambda: events(19.5, 32.1, 27.7, 31.6))
     step("prod_u3", lambda: products(0, 1))
-    step("ev5", lambda: events(99, 36.5))
-    step("lprod_u3", lambda: products(1, 1))
+    step("ev5", lambda: events(99, 40.4, 36.2, 40.1))
+    step("second", lambda: second(0))
+    step("lprod_u3", lambda: products(1, 1), jnp.logical_not(late_home))
+    step("ev6", lambda: events(99, 44.5, 44.6, 44.4))
+    step("lprod_u3o", lambda: products(1, 1), late_home)
+    step("x_final", x_final)
+    step("ev7", lambda: events(99, 48.7, 44.6, 48.5))
     step("lprod_u4", lambda: products(1, 0))
-    step("second", lambda: second(0))
-    step("ev6", lambda: events(99, 44.5))
+    step("ev8", lambda: events(99, 53.0, 48.9, 52.8))
     step("lprod_u2", lambda: product(1, 0, 1))
-    step("x_final", x_final)
     step("second_l", lambda: second(1))
-    step("ev7", lambda: events(99, 48.5))
     step("choose_send", choose_send)
     step("diag_upper", diag_upper)
-    step("ev8", lambda: events(99, 99))
+    step("ev9", lambda: events(99, 99, 99, 99))
     step("lprod_u1", lambda: product(1, 0, 0))
     step("choose_take", choose_take)
     step("crossed", crossed)
@@ -622,6 +698,19 @@
     step("finish", finish)
 
 
+def hand_out(*refs):
+    k = (len(refs) - 2) // 3
+    ins, outs, held = refs[:k], refs[k : 2 * k], refs[2 * k : 3 * k]
+    in_s, out_s = refs[3 * k :]
+    for i in range(k):
+        pltpu.make_async_copy(ins[i], held[i], in_s.at[i]).start()
+    for i in range(k):
+        pltpu.make_async_copy(ins[i], held[i], in_s.at[i]).wait()
+        pltpu.make_async_copy(held[i], outs[i], out_s.at[i]).start()
+    for i in range(k):
+        pltpu.make_async_copy(held[i], outs[i], out_s.at[i]).wait()
+
+
 def on_device(G, R, C, a, lu, mu, du, ll, ml, par, lp, dl):
     h = lu.shape[0]
     n = G * R
@@ -636,7 +725,7 @@
     small = jax.ShapeDtypeStruct((B, B), BF)
     tall = jax.ShapeDtypeStruct((h, B), BF)
     vm = pltpu.VMEM
-    return pl.pallas_call(
+    made = pl.pallas_call(
         functools.partial(kernel, G, R, C),
         out_shape=(tall, small, tall, small, small),
         in_specs=[hbm, hbm, sm, hbm, hbm, sm, sm, hbm, hbm],
@@ -678,6 +767,14 @@
             collective_id=0, has_side_effects=True, vmem_limit_bytes=60 * 1024 * 1024
         ),
     )(a, lu, mu, du, ll, ml, par, lp, dl)
+    k = len(made)
+    return pl.pallas_call(
+        hand_out,
+        out_shape=tuple(jax.ShapeDtypeStruct(v.shape, v.dtype) for v in made),
+        in_specs=[hbm] * k,
+        out_specs=(hbm,) * k,
+        scratch_shapes=[vm(v.shape, v.dtype) for v in made] + [dma((k,)), dma((k,))],
+    )(*made)
 
 
 def solution(mesh):

time: 124 us -> 100 us (0.81)
  Pallas kernels: 114 us -> 97.5 us
  local copies, waits for them, and re-layouts: 8.23 us -> 0 us
    pallas_call x1, Pallas kernels: 114 us -> 95.4 us  [on_device(): pl.pallas_call(functools.partial(kernel, G, R, C), out_shape=(tall, small...]
    unnamed x5 -> x0, local copies, waits for them, and re-layouts: 8.23 us -> none
    pallas_call x0 -> x1, Pallas kernels: none -> 2.09 us  [on_device(): pl.pallas_call(hand_out, out_shape=tuple((jax.ShapeDtypeStruct(v.shape, v...]
where the time goes in v2:
time: 100 us; the launch traced here: 98.1 us
  Pallas kernels  97.5 us (98%)
    pallas_call x1, Pallas kernels, on_device(): pl.pallas_call(functools.partial(kernel, G, R, C), out_shape=(tall, small...  95.4 us
    pallas_call x1, Pallas kernels, on_device(): pl.pallas_call(hand_out, out_shape=tuple((jax.ShapeDtypeStruct(v.shape, v...  2.09 us

profile of v2, /device:TPU:0, one launch (start us, length us, event | category | flops | bytes accessed | tf_op | source)
XLA Modules:
  0.0 98.1 jit_solution(14064136796362937831)
XLA Ops:
  0.6 95.4 %shard_map.128 = (bf16[768,256]{1,0:T(8,128)(2,1)}, bf16[256,256]{1,0:T(8,128)(2,1)}, bf16[768,256]{1,0:T(8,128)(2,1)}, bf16[256,256]{1,0:T(8,128)(2,1)}, bf16[256,256]{1,0:T(8,128)(2,1)}) custom-call(bf16[768,1536]{1,0:T(8,128)(2,1)} %a_in.1, bf16[768,256]{1,0:T(8,128)(2,1)} %lu_in.1, s32[4,24]{1,0:T(4,128)} %mu_ref.1, f32[256,256]{1,0:T(8,128)} %du_in.1, ...), custom_call_target="tpu_custom_call" | custom-call | tf_op jit(solution)/shard_map/pallas_call | solution.py:728
  96.0 2.1 %shard_map.129 = (bf16[768,256]{1,0:T(8,128)(2,1)}, bf16[256,256]{1,0:T(8,128)(2,1)}, bf16[768,256]{1,0:T(8,128)(2,1)}, bf16[256,256]{1,0:T(8,128)(2,1)}, bf16[256,256]{1,0:T(8,128)(2,1)}) custom-call(bf16[768,256]{1,0:T(8,128)(2,1)} %get-tuple-element.10.refs_0_, bf16[256,256]{1,0:T(8,128)(2,1)} %get-tuple-element.11.refs_1_, ...), custom_call_target="tpu_custom_call" | custom-call | tf_op jit(solution)/shard_map/pallas_call | solution.py:771

commit v3 on v2

--- a/solution.py
+++ b/solution.py
@@ -25,6 +25,11 @@
 
 
 TAU = 1.4
+HI, HO, AI, AO = range(4)
+OWN, AWAY_OWN, TRANSIT, ARRIVE = range(4)
+HOME, AWAY = range(2)
+FAR, NEAR = range(2)
+ALONG, CROSS, THROUGH = range(3)
 
 
 def plan(kind, R, q, CX, W):
@@ -38,114 +43,113 @@
         add(t, name, *args, slope=0.001)
 
     others = range(1, CX)
-    inner = kind[1] == "I"
+    inner = kind in (HI, AI)
+    at_home = kind in (HI, HO)
     if CX != 2:
         for p, l in ((0, 0), (0, 1), (1, 0), (1, 1)):
-            if kind[0] == "H":
-                for part in ("far", "near"):
-                    at(0, "own", p, l, part)
+            if at_home:
+                for part in (FAR, NEAR):
+                    at(0, OWN, p, l, part)
             else:
-                at(0, "away", p, l)
+                at(0, AWAY_OWN, p, l)
         for p in range(2):
             for s in range(1, R):
                 for side in range(2):
-                    at(1 + p + s / R, "transit", p, s, side)
+                    at(1 + p + s / R, TRANSIT, p, s, side)
             t = (5, 33)[p]
-            if kind[0] == "H":
-                for part in ("far", "near"):
+            if at_home:
+                for part in (FAR, NEAR):
                     for o in others:
                         for l in range(2):
-                            at(t, "arrive", p, "home", 0, o, l, part)
+                            at(t, ARRIVE, p, HOME, 0, o, l, part)
             for l in range(2):
                 for o in range(CX):
-                    for i in range(0 if kind[0] == "A" else 1, q):
-                        at(t + 1 + l + 0.1 * o, "arrive", p, ("away" if kind[0] == "A" else "home"), i, o, l, "far")
+                    for i in range(1 if at_home else 0, q):
+                        at(t + 1 + l + 0.1 * o, ARRIVE, p, AWAY if not at_home else HOME, i, o, l, FAR)
         return sorted(ev, key=lambda e: e[0])
-    if kind[0] == "H":
-        at(0, "own", 0, 0, "far")
+    if at_home:
+        at(0, OWN, 0, 0, FAR)
         for s in range(1, R):
             for side in range(2):
-                add((0 if inner else 0.1) + 3.9 * s, "transit", 0, s, side)
-                add(9.1 + 4 * s if inner else 25.2 + 4.1 * s, "transit", 1, s, side)
+                add((0 if inner else 0.1) + 3.9 * s, TRANSIT, 0, s, side)
+                add(9.1 + 4 * s if inner else 16.5 + 4.2 * s, TRANSIT, 1, s, side)
         if inner:
-            at(7, "own", 0, 1, "far")
-            at(12.2, "own", 0, 0, "near")
-            at(12.6, "own", 0, 1, "near")
-            at(24.8, "own", 1, 1, "far")
-            at(28.7, "own", 1, 0, "far")
-            at(28.8, "own", 1, 1, "near")
-            at(28.9, "own", 1, 0, "near")
+            add(4.03, OWN, 0, 1, FAR)
+            at(20.4, OWN, 0, 0, NEAR)
+            at(20.3, OWN, 0, 1, NEAR)
+            at(24.8, OWN, 1, 1, FAR)
+            at(28.7, OWN, 1, 0, FAR)
+            at(28.8, OWN, 1, 1, NEAR)
+            at(28.9, OWN, 1, 0, NEAR)
         else:
-            at(0.1, "own", 0, 0, "near")
-            add(4.0, "own", 0, 1, "far")
-            add(4.01, "own", 0, 1, "near")
-            at(18.2, "own", 1, 1, "far")
-            at(18.3, "own", 1, 1, "near")
-            at(18.4, "own", 1, 0, "far")
-            at(18.5, "own", 1, 0, "near")
+            at(0.1, OWN, 0, 0, NEAR)
+            add(4.0, OWN, 0, 1, FAR)
+            add(4.01, OWN, 0, 1, NEAR)
+            at(18.2, OWN, 1, 1, FAR)
+            at(18.3, OWN, 1, 1, NEAR)
+            at(18.4, OWN, 1, 0, FAR)
+            at(18.5, OWN, 1, 0, NEAR)
         for o in others:
-            add(4.05, "arrive", 0, "home", 0, o, 0, "far")
-            add(8.0, "arrive", 0, "home", 0, o, 1, "far")
+            add(4.05, ARRIVE, 0, HOME, 0, o, 0, FAR)
+            add(8.0, ARRIVE, 0, HOME, 0, o, 1, FAR)
             if inner:
-                at(12.4, "arrive", 0, "home", 0, o, 0, "near")
-                at(12.8, "arrive", 0, "home", 0, o, 1, "near")
-                at(17, "arrive", 1, "home", 0, o, 1, "far")
-                at(19.9, "arrive", 1, "home", 0, o, 0, "far")
-                at(25, "arrive", 1, "home", 0, o, 1, "near")
-                at(25.1, "arrive", 1, "home", 0, o, 0, "near")
+                at(12.4, ARRIVE, 0, HOME, 0, o, 0, NEAR)
+                at(12.8, ARRIVE, 0, HOME, 0, o, 1, NEAR)
+                at(17, ARRIVE, 1, HOME, 0, o, 1, FAR)
+                at(19.9, ARRIVE, 1, HOME, 0, o, 0, FAR)
+                at(20.35, ARRIVE, 1, HOME, 0, o, 1, NEAR)
+                at(25.1, ARRIVE, 1, HOME, 0, o, 0, NEAR)
             else:
-                add(8.01, "arrive", 0, "home", 0, o, 1, "near")
-                at(11.5, "arrive", 0, "home", 0, o, 0, "near")
-                add(15.2, "arrive", 1, "home", 0, o, 1, "far")
-                add(15.21, "arrive", 1, "home", 0, o, 1, "near")
-                at(20.2, "arrive", 1, "home", 0, o, 0, "far")
-                at(20.3, "arrive", 1, "home", 0, o, 0, "near")
+                add(8.01, ARRIVE, 0, HOME, 0, o, 1, NEAR)
+                at(11.5, ARRIVE, 0, HOME, 0, o, 0, NEAR)
+                add(15.2, ARRIVE, 1, HOME, 0, o, 1, FAR)
+                add(15.21, ARRIVE, 1, HOME, 0, o, 1, NEAR)
+                at(20.2, ARRIVE, 1, HOME, 0, o, 0, FAR)
+                at(20.3, ARRIVE, 1, HOME, 0, o, 0, NEAR)
         for i in range(1, q):
-            first = (4.02, 9.0, 12.5, 16.5) if inner else (16.5, 25.0, 29.2, 20.8)
-            last = (29.2, 25.0, 20.7, 33.5) if inner else (54.3, 50.1, 41.6, 45.8)
+            first = (15.4, 10.9, 12.5, 16.5) if inner else (41.6, 33.2, 20.5, 16.2)
+            last = (29.2, 25.0, 20.7, 33.5) if inner else (54.3, 50.1, 37.4, 45.8)
             for p, (t1, t2, t3, t4) in ((0, first), (1, last)):
-                add(t1, "arrive", p, "home", i, 0, 0, "far")
-                add(t2, "arrive", p, "home", i, 0, 1, "far")
+                flat = 0.001 if inner and p == 0 else TAU
+                add(t1, ARRIVE, p, HOME, i, 0, 0, FAR, slope=flat)
+                add(t2, ARRIVE, p, HOME, i, 0, 1, FAR, slope=flat)
                 for o in others:
-                    add(t3, "arrive", p, "home", i, o, 1, "far")
-                    add(t4, "arrive", p, "home", i, o, 0, "far")
+                    add(t3, ARRIVE, p, HOME, i, o, 1, FAR)
+                    add(t4, ARRIVE, p, HOME, i, o, 0, FAR)
     else:
-        at(0, "away", 0, 0)
+        at(0, AWAY_OWN, 0, 0)
         for s in range(1, R):
             for side in range(2):
-                add(0.1 + 3.9 * s, "transit", 0, s, side)
-                add(11.5 + 3.9 * s, "transit", 1, s, side)
-        add(4.1, "away", 0, 1)
-        add(8.5, "away", 1, 1)
-        at(11.6, "away", 1, 0)
+                add(0.1 + 3.9 * s, TRANSIT, 0, s, side)
+                add(11.5 + 3.9 * s, TRANSIT, 1, s, side)
+        add(4.1, AWAY_OWN, 0, 1)
+        add(8.5, AWAY_OWN, 1, 1)
+        at(11.6, AWAY_OWN, 1, 0)
         d = 0 if inner else 3.9
         for i in range(q):
-            add(4.05 + d + 3.95 * i, "arrive", 0, "away", i, 0, 0, "far")
-            add(12.1 + d + 8.5 * i, "arrive", 0, "away", i, 0, 1, "far")
-            add(37.5 + d + 4.2 * i, "arrive", 1, "away", i, 0, 1, "far")
-            add(46 + d + 4.2 * i, "arrive", 1, "away", i, 0, 0, "far")
+            add(4.05 + d + 20.75 * i, ARRIVE, 0, AWAY, i, 0, 0, FAR)
+            add(8.0 + d + 8.4 * i, ARRIVE, 0, AWAY, i, 0, 1, FAR)
+            add(37.5 + d + 4.2 * i, ARRIVE, 1, AWAY, i, 0, 1, FAR)
+            add(46 + d + 4.2 * i, ARRIVE, 1, AWAY, i, 0, 0, FAR)
             for o in others:
-                add(8.2 + d + 4 * i, "arrive", 0, "away", i, o, 0, "far")
-                add(16.4 + d + 8.4 * i, "arrive", 0, "away", i, o, 1, "far")
-                if inner:
-                    at(27.9 + 0.1 * i, "arrive", 1, "away", i, o, 0, "far")
-                else:
-                    add(37.2 + 4.2 * i, "arrive", 1, "away", i, o, 0, "far")
-                add(29 + d + 4.2 * i, "arrive", 1, "away", i, o, 1, "far")
+                add(8.2 + d + 4 * i, ARRIVE, 0, AWAY, i, o, 0, FAR)
+                add(12.1 + d + 8.5 * i, ARRIVE, 0, AWAY, i, o, 1, FAR)
+                at((36.1 if inner else 36.3) + 0.01 * i, ARRIVE, 1, AWAY, i, o, 0, FAR)
+                add(29 + d + 4.2 * i, ARRIVE, 1, AWAY, i, o, 1, FAR)
     return sorted(ev, key=lambda e: e[0])
 
 
 def kernel(
     G, R, C,
-    a_in, lu_in, mu_ref, du_in, ll_in, ml_ref, par_ref, lp_in, dl_in,
+    a_in, lu_in, mu_in, du_in, ll_in, ml_in, par_in, lp_in, dl_in,
     x_out, diagu_out, y_out, yp_out, diagl_out,
-    a_ref, lu_ref, ll_ref, du_ref, dl_ref, lp_ref,
+    a_ref, lu_ref, ll_ref, du_ref, dl_ref, lp_ref, mu_ref, ml_ref, par_ref,
     x_ref, y_ref, ybuf, zbuf, col, acc, part, near_y, near_x, sent_y, sent_x, last_y, last_x,
-    rhs, lum, llm, xrow, selbuf, chy, chosen, part3, red, dufull, dpar, ypfull, back, dlfull,
+    rhs, lum, llm, xrow, yrow, sel_y, ch_y, sel_x, ch_x, chosen, part3, red, dufull, dpar, ypfull, back, dlfull,
     linked, terms, in_s, out_s,
     h_ss, h_rs, t_ss, t_rs, c_rs, v_ss, r_ss, x_ss,
     ny_ss, ny_rs, nx_ss, nx_rs, ly_ss, ly_rs, lx_ss, lx_rs,
-    xr_ss, xr_rs, ch_ss, ch_rs,
+    k_ss, xr_rs, yr_rs, cy_rs, cx_rs,
     red_ss, red_rs, s_ss, s_rs,
 ):
     g, z, c = lax.axis_index("grp"), lax.axis_index("row"), lax.axis_index("col")
@@ -182,7 +186,10 @@
     ins = [
         pltpu.make_async_copy(src, dst, in_s.at[i])
         for i, (src, dst) in enumerate(
-            ((lu_in, lu_ref), (ll_in, ll_ref), (a_in, a_ref), (lp_in, lp_ref), (du_in, du_ref), (dl_in, dl_ref))
+            (
+                (lu_in, lu_ref), (ll_in, ll_ref), (mu_in, mu_ref), (ml_in, ml_ref), (par_in, par_ref),
+                (a_in, a_ref), (lp_in, lp_ref), (du_in, du_ref), (dl_in, dl_ref),
+            )
         )
     ]
     barrier = pltpu.get_barrier_semaphore()
@@ -194,10 +201,9 @@
         )
     for i in ins:
         i.start()
-    ins[0].wait()
-    ins[1].wait()
-    with jax.named_scope("barrier"):
-        pl.semaphore_wait(barrier, n - 1 + C - 1)
+    for i in ins[:2]:
+        i.wait()
+    pl.semaphore_wait(barrier, n - 1 + C - 1)
 
     log = []
 
@@ -229,7 +235,7 @@
         return col.at[p, j * C + u, cut(w), :]
 
     def along(p, j, u, side, w, src):
-        return ("v", p, side), lambda: copy(
+        return (ALONG, p, side), lambda: copy(
             src, at_col(p, j, u, w), v_ss.at[p, side], c_rs.at[p, j * C + u, w], side_dev(side)
         )
 
@@ -240,13 +246,13 @@
 
     def cross(p, z0, l, w, src):
         u, j = col_u(0, l), lax.rem(z0, q)
-        return ("x", p, 0), lambda: copy(
+        return (CROSS, p, 0), lambda: copy(
             src, at_col(p, j, u, w), x_ss.at[p, 0], c_rs.at[p, j * C + u, w],
             pdev(y, lax.div(z0, q)),
         )
 
     def through(p, z0, side, w, src):
-        return ("t", p, side), lambda: copy(
+        return (THROUGH, p, side), lambda: copy(
             src, zbuf.at[p, z0, cut(w), :], t_ss.at[p, side], t_rs.at[p, z0, w], side_dev(side)
         )
 
@@ -264,7 +270,7 @@
                 for k in range(2)
             ]
 
-        if part == "near":
+        if part == NEAR:
             return home, None, sides(True), None
 
         def local():
@@ -292,7 +298,7 @@
         return land(ok, path, b0 != x), through(p, z0, side, w, at)[1], outs, None
 
     def arrive(p, kind, i, o, l, part, w):
-        j = lax.rem(zj + i, q) if kind == "home" else jnp.where(z < x * q, i, q - 1 - i)
+        j = lax.rem(zj + i, q) if kind == HOME else jnp.where(z < x * q, i, q - 1 - i)
         z0 = x * q + j
         u = col_u(o, l)
         at = at_col(p, j, u, w)
@@ -301,18 +307,18 @@
         outs = []
         for k in range(2):
             step_to = along(p, j, u, k, w, at)
-            if kind == "away":
+            if kind == AWAY:
                 if not late:
                     outs.append((side[k], step_to))
             elif i == 0:
-                if part == "near":
+                if part == NEAR:
                     outs.append((land(side[k], near_side[k]), step_to))
                 elif not late:
                     outs.append((land(side[k], jnp.logical_not(near_side[k])), step_to))
             else:
                 outs.append((land(side[k], near_side[k]) if late else side[k], step_to))
-        live = home if kind == "home" else away
-        if part == "near":
+        live = home if kind == HOME else away
+        if part == NEAR:
             return live, None, outs, None
         outs.append((None, relay(p, j, u, w, at)))
         return live, relay(p, j, u, w, at)[1], outs, None
@@ -350,17 +356,17 @@
                         on = live if cond is None else land(live, cond)
                         count[key] = count.get(key, 0) + jnp.where(on, 1, 0)
         for (kind, p, side), number in sorted(count.items()):
-            sem = {"v": v_ss, "x": x_ss, "t": t_ss}[kind].at[p, side]
-            for k in range(1, {"v": q * C, "x": R + G, "t": R}[kind] + 1):
+            sem = (v_ss, x_ss, t_ss)[kind].at[p, side]
+            for k in range(1, (q * C, R + G, R)[kind] + 1):
                 pl.when(number == k)(lambda: wait_blocks(sem, p, k))
 
-    handlers = {"own": own, "away": away_own, "transit": transit, "arrive": arrive}
-    kinds = ("HI", "HO", "AI", "AO")
-    timed = {k: plan(k, R, q, CX, W) for k in kinds}
-    is_kind = {
-        "HI": land(home, jnp.logical_not(outer)), "HO": land(home, outer),
-        "AI": land(away, jnp.logical_not(outer)), "AO": land(away, outer),
-    }
+    handlers = (own, away_own, transit, arrive)
+    kinds = (HI, HO, AI, AO)
+    timed = [plan(k, R, q, CX, W) for k in kinds]
+    is_kind = (
+        land(home, jnp.logical_not(outer)), land(home, outer),
+        land(away, jnp.logical_not(outer)), land(away, outer),
+    )
 
     def events(*until):
         for k, to in zip(kinds, until):
@@ -499,31 +505,50 @@
         at = dpar.at[pl.ds(0, C - 1)]
         return copy(at, at, s_ss.at[3], s_rs.at[3], rdev(r))
 
-    def xr_copy(o, w):
+    TR = H2 // 2
+
+    def tile(t):
+        return pl.ds(t * TR, TR)
+
+    def low_tile(t):
+        return pl.ds(H2 + t * TR, TR)
+
+    def xr_copy(o, t):
         return copy(
-            x_ref.at[cut(w), :], xrow.at[CX - o, cut(w), :], xr_ss.at[0],
-            xr_rs.at[CX - o, w], pdev(y, xo(o)),
-        )
-
-    def ch_copy(w):
-        return copy(selbuf.at[cut(w), :], chy.at[cut(w), :], ch_ss.at[0], ch_rs.at[w], pdev(oy, x))
-
-    def pick(who, base, w):
-        v = base
+            x_ref.at[tile(t), :], xrow.at[CX - o, tile(t), :], k_ss.at[0], xr_rs.at[CX - o, t],
+            pdev(y, xo(o)),
+        )
+
+    def yr_copy(t):
+        return copy(x_ref.at[low_tile(t), :], yrow.at[tile(t), :], k_ss.at[1], yr_rs.at[t], pdev(oy, x))
+
+    def cy_copy(t):
+        return copy(sel_y.at[tile(t), :], ch_y.at[tile(t), :], k_ss.at[2], cy_rs.at[t], pdev(oy, x))
+
+    def cx_copy(o, t):
+        return copy(
+            sel_x.at[o, tile(t), :], ch_x.at[CX - o, tile(t), :], k_ss.at[3], cx_rs.at[CX - o, t],
+            pdev(y, xo(o)),
+        )
+
+    def pick_row(who, v, t):
         for o in range(CX):
-            src = x_ref if o == 0 else xrow.at[o]
-            v = jnp.where(who == y * CX + xo(o), src[cut(w), :], v)
+            block = x_ref[tile(t), :] if o == 0 else xrow[o, tile(t), :]
+            v = jnp.where(who == y * CX + xo(o), block, v)
         return v
+
+    def pick_pair(who, v, t):
+        v = jnp.where(who == oy * CX + x, yrow[tile(t), :], v)
+        return jnp.where(who == c, x_ref[low_tile(t), :], v)
 
     def out_copy(i, src, dst):
         return pltpu.make_async_copy(src, dst, out_s.at[i])
 
-    def step(name, f, cond=None):
-        with jax.named_scope(name):
-            if cond is None:
-                f()
-            else:
-                pl.when(cond)(f)
+    def step(f, cond=None):
+        if cond is None:
+            f()
+        else:
+            pl.when(cond)(f)
 
     def start_hops():
         for p in range(2):
@@ -531,6 +556,9 @@
                 hop_copy(p, w).start()
 
     def mask_own():
+        for i in ins[2:5]:
+            i.wait()
+
         @pl.loop(0, hb)
         def _(t):
             rows = pl.ds(pl.multiple_of(t * B, B), B)
@@ -542,20 +570,24 @@
         xt, xl = total(0)
         x_ref[top, :] = xt
         x_ref[low, :] = xl
-        for w in range(W):
+        for t in range(2):
             for o in range(1, CX):
-                xr_copy(o, w).start()
+                xr_copy(o, t).start()
+            yr_copy(t).start()
         out_copy(0, x_ref, x_out).start()
         part3[0] = tdot(lum[...], x_ref[...]).astype(BF)
         send_sum(0)
 
     def choose_send():
-        to = par_ref[oy * CX + x]
-        for w in range(W):
+        for t in range(2):
             for o in range(1, CX):
-                xr_copy(CX - o, w).wait_recv()
-            selbuf[cut(w), :] = pick(to, x_ref[cut(w), :], w)
-            ch_copy(w).start()
+                xr_copy(CX - o, t).wait_recv()
+            sel_y[tile(t), :] = pick_row(par_ref[oy * CX + x], x_ref[tile(t), :], t)
+            cy_copy(t).start()
+            yr_copy(t).wait_recv()
+            for o in range(1, CX):
+                sel_x[o, tile(t), :] = pick_pair(par_ref[y * CX + xo(o)], x_ref[low_tile(t), :], t)
+                cx_copy(o, t).start()
 
     def diag_upper():
         dslice = (du_ref[mine, :] - take_sum(0)).astype(BF)
@@ -565,12 +597,16 @@
             dp_copy(o).start()
         spread(0, dufull)
 
-    here = par_ref[c]
-
     def choose_take():
-        for w in range(W):
-            ch_copy(w).wait_recv()
-            chosen[cut(w), :] = pick(here, chy[cut(w), :], w)
+        here = par_ref[c]
+        for t in range(2):
+            cy_copy(t).wait_recv()
+            chosen[tile(t), :] = pick_row(here, ch_y[tile(t), :], t)
+            v = x_ref[low_tile(t), :]
+            for o in range(1, CX):
+                cx_copy(CX - o, t).wait_recv()
+                v = jnp.where(lax.rem(here, CX) == xo(o), ch_x[o, tile(t), :], v)
+            chosen[low_tile(t), :] = pick_pair(here, v, t)
 
     def crossed():
         part3[1] = tdot(chosen[...], llm[...]).astype(BF)
@@ -584,17 +620,20 @@
             acc[1, 0, rows, :] += v
             linked[rows, :] = v.astype(BF)
 
+        back[...] = tdot(linked[...], llm[...])
+
     def parent_terms():
         all_dp().wait_recv()
-        v = jnp.dot(dpar[here], lp_ref[...], preferred_element_type=F32)
+        v = jnp.dot(dpar[par_ref[c]], lp_ref[...], preferred_element_type=F32)
         terms[...] = v
-        back[...] = -tdot(linked[...], llm[...]) - tdot(lp_ref[mine, :], v.astype(BF))
+        part3[3] = tdot(lp_ref[mine, :], v.astype(BF)).astype(BF)
+        send_sum(3)
 
     def y_final():
         yt, yl = total(1)
         y_ref[top, :] = yt
         y_ref[low, :] = yl
-        part3[2] = (tdot(llm[...], y_ref[...]) + back[...]).astype(BF)
+        part3[2] = (tdot(llm[...], y_ref[...]) - back[...]).astype(BF)
         send_sum(2)
         out_copy(1, y_ref, y_out).start()
 
@@ -603,7 +642,7 @@
         spread(1, ypfull)
 
     def diag_lower():
-        dlfull[mine, :] = (dl_ref[mine, :] - take_sum(2)).astype(BF)
+        dlfull[mine, :] = (dl_ref[mine, :] - take_sum(2) + take_sum(3)).astype(BF)
         spread(2, dlfull)
 
     def gather_upper():
@@ -619,7 +658,7 @@
         out_copy(4, dlfull, diagl_out).start()
 
     def wait_ins():
-        for i in ins[2:]:
+        for i in ins[5:]:
             i.wait()
 
     def products(p, l):
@@ -627,43 +666,57 @@
             product(p, o, l)
 
     pl.when(jnp.logical_not(primary))(start_hops)
-    late_home = is_kind["HO"]
-    step("ev0", lambda: events(0.1, 0.2, 0.1, 0.1))
-    step("mask", mask_own)
-    step("ev1", lambda: events(11.9, 19.5, 10.9, 14.9))
+    ho, hi = is_kind[HO], is_kind[HI]
+    no = jnp.logical_not(ho)
+    step(lambda: events(0.1, 0.2, 0.1, 0.1))
+    step(mask_own)
+    step(lambda: events(15.5, 19.1, 15.1, 19.0))
     wait_ins()
-    step("prod_u1", lambda: product(0, 0, 0))
-    step("ev2", lambda: events(19.5, 23.9, 15.1, 19.0))
-    step("prod_u4", lambda: products(0, 0))
-    step("ev3", lambda: events(19.5, 28.0, 23.5, 27.4))
-    step("prod_u2", lambda: product(0, 0, 1))
-    step("ev4", lambda: events(19.5, 32.1, 27.7, 31.6))
-    step("prod_u3", lambda: products(0, 1))
-    step("ev5", lambda: events(99, 40.4, 36.2, 40.1))
-    step("second", lambda: second(0))
-    step("lprod_u3", lambda: products(1, 1), jnp.logical_not(late_home))
-    step("ev6", lambda: events(99, 44.5, 44.6, 44.4))
-    step("lprod_u3o", lambda: products(1, 1), late_home)
-    step("x_final", x_final)
-    step("ev7", lambda: events(99, 48.7, 44.6, 48.5))
-    step("lprod_u4", lambda: products(1, 0))
-    step("ev8", lambda: events(99, 53.0, 48.9, 52.8))
-    step("lprod_u2", lambda: product(1, 0, 1))
-    step("second_l", lambda: second(1))
-    step("choose_send", choose_send)
-    step("diag_upper", diag_upper)
-    step("ev9", lambda: events(99, 99, 99, 99))
-    step("lprod_u1", lambda: product(1, 0, 0))
-    step("choose_take", choose_take)
-    step("crossed", crossed)
-    step("coupling", coupling)
-    step("parent_terms", parent_terms)
-    step("y_final", y_final)
-    step("y_parent", y_parent)
-    step("diag_lower", diag_lower)
-    step("gather_upper", gather_upper)
-    step("gather_parent", gather_parent)
-    step("gather_lower", gather_lower)
+    step(lambda: products(0, 1), hi)
+    step(lambda: product(0, 0, 1), hi)
+    step(lambda: product(0, 0, 0), hi)
+    step(lambda: events(20.5, 19.1, 15.1, 19.0))
+    step(lambda: products(0, 0))
+    step(lambda: events(20.5, 23.4, 19.3, 23.2))
+    step(lambda: product(0, 0, 1), away)
+    step(lambda: products(0, 1), ho)
+    step(lambda: events(20.5, 30.0, 23.5, 27.4))
+    step(lambda: products(0, 1), away)
+    step(lambda: events(20.5, 36.1, 27.7, 31.6))
+    step(lambda: product(0, 0, 0), away)
+    step(lambda: product(0, 0, 1), ho)
+    step(lambda: events(25.3, 36.1, 33.0, 31.6))
+    step(lambda: second(0))
+    step(lambda: events(99, 40.3, 36.2, 36.4))
+    step(lambda: products(1, 0), no)
+    step(lambda: events(99, 40.3, 36.2, 40.1))
+    step(lambda: products(1, 1))
+    step(lambda: events(99, 44.5, 44.6, 44.4))
+    step(lambda: product(0, 0, 0), ho)
+    step(x_final)
+    step(lambda: events(99, 48.7, 44.6, 48.5))
+    step(lambda: product(1, 0, 1), no)
+    step(lambda: second(1), no)
+    step(lambda: products(1, 0), ho)
+    step(choose_send, ho)
+    step(lambda: events(99, 53.0, 48.9, 52.8))
+    step(choose_send, no)
+    step(diag_upper, is_kind[AO])
+    step(lambda: product(1, 0, 1), ho)
+    step(lambda: second(1), ho)
+    step(lambda: events(99, 99, 99, 99))
+    step(diag_upper, jnp.logical_not(is_kind[AO]))
+    step(lambda: product(1, 0, 0))
+    step(choose_take)
+    step(crossed)
+    step(coupling)
+    step(y_final)
+    step(parent_terms)
+    step(y_parent)
+    step(diag_lower)
+    step(gather_upper)
+    step(gather_parent)
+    step(gather_lower)
 
     def finish():
         @pl.when(primary)
@@ -683,9 +736,11 @@
             sent(nx_ss.at[p], near_x.at[p, pl.ds(0, (CX - 1) * G)])
             sent(ly_ss.at[p], last_y.at[p, pl.ds(0, CX - 1)])
             sent(lx_ss.at[p], last_x.at[p])
-        sent(xr_ss.at[0], xrow.at[pl.ds(0, CX - 1)])
-        sent(ch_ss.at[0], chy)
-        for k in range(3):
+        sent(k_ss.at[0], xrow.at[pl.ds(0, CX - 1)])
+        sent(k_ss.at[1], yrow)
+        sent(k_ss.at[2], ch_y)
+        sent(k_ss.at[3], ch_x.at[pl.ds(0, CX - 1)])
+        for k in range(4):
             all_red(k).wait_send()
         for i, buf in enumerate((dufull, ypfull, dlfull)):
             all_spread(i, buf).wait_send()
@@ -695,7 +750,7 @@
         ):
             out_copy(i, src, dst).wait()
 
-    step("finish", finish)
+    step(finish)
 
 
 def hand_out(*refs):
@@ -720,7 +775,6 @@
     W = h // B
     H2 = h // 2
     hbm = pl.BlockSpec(memory_space=pl.ANY)
-    sm = pl.BlockSpec(memory_space=pltpu.SMEM)
     dma = pltpu.SemaphoreType.DMA
     small = jax.ShapeDtypeStruct((B, B), BF)
     tall = jax.ShapeDtypeStruct((h, B), BF)
@@ -728,10 +782,11 @@
     made = pl.pallas_call(
         functools.partial(kernel, G, R, C),
         out_shape=(tall, small, tall, small, small),
-        in_specs=[hbm, hbm, sm, hbm, hbm, sm, sm, hbm, hbm],
+        in_specs=[hbm] * 9,
         out_specs=(hbm,) * 5,
         scratch_shapes=[
             vm(a.shape, BF), vm((h, B), BF), vm((h, B), BF), vm((B, B), F32), vm((B, B), F32), vm((B, B), BF),
+            pltpu.SMEM(mu.shape, mu.dtype), pltpu.SMEM(ml.shape, ml.dtype), pltpu.SMEM(par.shape, par.dtype),
             vm((h, B), BF), vm((h, B), BF),
             vm((2, h, B), BF),
             vm((2, R, h, B), BF),
@@ -746,22 +801,23 @@
             vm((2, H2, B), BF),
             vm((q * h, B), BF),
             vm((h, B), BF), vm((h, B), BF),
-            vm((CX, h, B), BF), vm((h, B), BF), vm((h, B), BF), vm((h, B), BF),
-            vm((3, B, B), BF),
-            vm((3, n, S, B), BF),
+            vm((CX, H2, B), BF), vm((H2, B), BF), vm((H2, B), BF), vm((H2, B), BF),
+            vm((CX, H2, B), BF), vm((CX, H2, B), BF), vm((h, B), BF),
+            vm((4, B, B), BF),
+            vm((4, n, S, B), BF),
             vm((B, B), BF),
             vm((C, S, B), BF),
             vm((B, B), BF),
             vm((B, B), F32),
             vm((B, B), BF),
             vm((h, B), BF), vm((S, B), F32),
-            dma((6,)), dma((5,)),
+            dma((9,)), dma((5,)),
             dma((2,)), dma((2, W)), dma((2, 2)), dma((2, R, W)),
             dma((2, q * C, W)), dma((2, 2)), dma((2,)), dma((2, 1)),
             dma((2,)), dma((2, CX)), dma((2,)), dma((2, CX * G)),
             dma((2,)), dma((2, CX)), dma((2,)), dma((2,)),
-            dma((1,)), dma((CX, W)), dma((1,)), dma((W,)),
-            dma((3,)), dma((3,)), dma((4,)), dma((4,)),
+            dma((4,)), dma((CX, 2)), dma((2,)), dma((2,)), dma((CX, 2)),
+            dma((4,)), dma((4,)), dma((4,)), dma((4,)),
         ],
         compiler_params=pltpu.CompilerParams(
             collective_id=0, has_side_effects=True, vmem_limit_bytes=60 * 1024 * 1024

time: 100 us -> 90.9 us (0.909); the launches traced: 98.1 us -> 90.8 us
  Pallas kernels: 97.5 us -> 90 us
    pallas_call x1, Pallas kernels: 95.4 us -> 87.9 us  [on_device(): pl.pallas_call(functools.partial(kernel, G, R, C), out_shape=(tall, small...]
where the time goes in v3:
time: 90.9 us; the launch traced here: 90.8 us
  Pallas kernels  90 us (99%)
    pallas_call x1, Pallas kernels, on_device(): pl.pallas_call(functools.partial(kernel, G, R, C), out_shape=(tall, small...  87.9 us
    pallas_call x1, Pallas kernels, on_device(): pl.pallas_call(hand_out, out_shape=tuple((jax.ShapeDtypeStruct(v.shape, v...  2.09 us

profile of v3, /device:TPU:0, one launch (start us, length us, event | category | flops | bytes accessed | tf_op | source)
XLA Modules:
  0.0 90.8 jit_solution(10179612245559243116)
XLA Ops:
  0.6 87.9 %shard_map.128 = (bf16[768,256]{1,0:T(8,128)(2,1)}, bf16[256,256]{1,0:T(8,128)(2,1)}, bf16[768,256]{1,0:T(8,128)(2,1)}, bf16[256,256]{1,0:T(8,128)(2,1)}, bf16[256,256]{1,0:T(8,128)(2,1)}) custom-call(bf16[768,1536]{1,0:T(8,128)(2,1)} %a_in.1, bf16[768,256]{1,0:T(8,128)(2,1)} %lu_in.1, s32[4,24]{1,0:T(4,128)} %mu_in.1, f32[256,256]{1,0:T(8,128)} %du_in.1, ...), custom_call_target="tpu_custom_call" | custom-call | tf_op jit(solution)/shard_map/pallas_call | solution.py:782
  88.5 2.1 %shard_map.129 = (bf16[768,256]{1,0:T(8,128)(2,1)}, bf16[256,256]{1,0:T(8,128)(2,1)}, bf16[768,256]{1,0:T(8,128)(2,1)}, bf16[256,256]{1,0:T(8,128)(2,1)}, bf16[256,256]{1,0:T(8,128)(2,1)}) custom-call(bf16[768,256]{1,0:T(8,128)(2,1)} %get-tuple-element.10.refs_0_, bf16[256,256]{1,0:T(8,128)(2,1)} %get-tuple-element.11.refs_1_, ...), custom_call_target="tpu_custom_call" | custom-call | tf_op jit(solution)/shard_map/pallas_call | solution.py:827
